TPU v7x, 256 devices: a whole 4x4x8 slice. The times are simulated.
256 devices in a mesh: toa: 128 (over z, y, x), rep: 2 (over core).
Axes of the slice: x: 4, y: 4, z: 8, core: 2. Of those that a mesh axis runs over, the one named last changes fastest.
Arguments:
- residual: float32 [16384, 256], P('toa'), may hold values from -6 to 6
- toa_error: float32 [16384, 256], P('toa'), may hold values from 0.3 to 3
- basis_rows: bfloat16 [16384, 100, 256], P('toa', 'rep'), may hold values from -0.041432038 to 0.041432038
- efac_table: float32 [128, 64], replicated, may hold values from 0.5 to 2
- equad_table: float32 [128, 64], replicated, may hold values from 0.1 to 1
- pulsar: int32 [16384], P('toa'), may hold values from 0 to 127
- backend: int32 [16384], P('toa'), may hold values from 0 to 63
- counts: int32 [16384], P('toa'), may hold values from 64 to 256
- owner_slot: int32 [16384], P('toa'), may hold values from 0 to 16383, as said below
Outputs:
- gram_matrix: float32 [128, 100, 100], P('toa', None, 'rep')
- projection: float32 [128, 100], P('toa', 'rep')
- whitened: float32 [16384, 256], P('toa')
Inputs may be any that keep to these rules, and one draw needn't show every extreme that they name: A permutation of the 16384 slots, independent of pulsar and backend; owner_slot // 128 is the device index along toa that holds the tile's output row and owner_slot % 128 its place there; each device's tiles go exactly 1 to each device.
All inputs are finite; a program needn't handle non-finite values.
Results may differ from a plain program's by a relative error of at most 0.0032.
Values may be sent and summed in bfloat16 or wider, within the bound.
No kernel may reach another device: no remote copies, remote signals or barrier semaphores. Data moves between devices by JAX's collectives and lax.ppermute only.
A program may use at most 64 MiB of HBM per device.

v0:
```python
import jax
import jax.numpy as jnp
from jax import lax
from jax.sharding import Mesh
from jax.sharding import PartitionSpec as P

TOA = ("toa_0", "toa_1", "toa_2")


def in_blocks(value, dim, peers):
    shape = value.shape
    pieces = value.reshape(*shape[:dim], peers, shape[dim] // peers, *shape[dim + 1 :])
    return jnp.moveaxis(pieces, dim, 0)


def sum_at_owner(value, axis, dim):
    peers = lax.axis_size(axis)
    pieces = lax.all_to_all(in_blocks(value, dim, peers), axis, 0, 0, tiled=True)
    return jnp.sum(pieces, axis=0)


def summed_rows(value, axes, dim):
    far, near = axes
    own = sum_at_owner(in_blocks(value, dim, lax.axis_size(far)), near, dim + 1)
    return jnp.sum(lax.all_to_all(own, far, 0, 0, tiled=True), axis=0)


def side_by_side(arrays, axis, dim, along):
    columns = [a.reshape(*a.shape[:along], -1) for a in arrays]
    both = jnp.concatenate(columns, axis=along)
    filled, at, done = (summed_rows(both, axis, dim), 0, [])
    for a, column in zip(arrays, columns):
        section = filled[..., at : at + column.shape[along]]
        done.append(section.reshape(*section.shape[:along], *a.shape[along:]))
        at += column.shape[along]
    return tuple(done)


def sent_together(arrays, axis, split_dim, concat_dim, along):
    ends, at = ([], 0)
    for a in arrays[:-1]:
        at += a.shape[along]
        ends.append(at)
    both = jnp.concatenate(arrays, axis=along)
    return tuple(
        jnp.split(
            lax.all_to_all(both, axis, split_axis=split_dim, concat_axis=concat_dim, tiled=True),
            ends,
            axis=along,
        )
    )


def lookup(small_table, onehot_pulsar, onehot_backend):
    table_rows = jnp.dot(onehot_pulsar, small_table, precision=lax.Precision.HIGHEST)
    return jnp.sum(table_rows * onehot_backend, axis=1)


def tile_weights(residual, toa_error, pulsar, backend, counts, efac_table, equad_table):
    onehot_pulsar = (
        pulsar[:, None] == jnp.arange(efac_table.shape[0], dtype=jnp.int32)[None, :]
    ).astype(jnp.float32)
    onehot_backend = (
        backend[:, None] == jnp.arange(efac_table.shape[1], dtype=jnp.int32)[None, :]
    ).astype(jnp.float32)
    factor = lookup(efac_table, onehot_pulsar, onehot_backend)
    floor_term = lookup(equad_table, onehot_pulsar, onehot_backend)
    valid_rows = jnp.arange(residual.shape[1], dtype=jnp.int32)[None, :] < counts[:, None]
    weight = jnp.where(
        valid_rows, 1.0 / (factor[:, None] ** 2 * toa_error**2 + floor_term[:, None] ** 2), 0.0
    )
    return (onehot_pulsar, weight)


def pulsar_terms(basis_own, weight, residual, onehot_pulsar):
    scaled = (weight[:, None, :] * basis_own).astype(jnp.bfloat16)
    weighted_res = (weight * residual).astype(jnp.bfloat16)
    tile_gram = jnp.einsum(
        "tkr,tjr->tkj",
        lax.all_gather(basis_own, "rep", axis=1, tiled=True),
        scaled,
        preferred_element_type=jnp.float32,
    )
    tile_proj = jnp.einsum(
        "tjr,tr->tj", basis_own, weighted_res, preferred_element_type=jnp.float32
    )
    tile_total, full_width, half_width = tile_gram.shape
    pulsar_total = onehot_pulsar.shape[1]
    gram_part = jnp.dot(
        onehot_pulsar.T,
        tile_gram.reshape(tile_total, full_width * half_width),
        precision=lax.Precision.HIGHEST,
    )
    gram_part = gram_part.reshape(pulsar_total, full_width, half_width)
    proj_part = jnp.dot(onehot_pulsar.T, tile_proj, precision=lax.Precision.HIGHEST)
    return side_by_side((gram_part, proj_part), ("toa_0", ("toa_1", "toa_2")), 0, 1)


def shards(
    residual, toa_error, basis_rows, efac_table, equad_table, pulsar, backend, counts, owner_slot
):
    tile_count = residual.shape[0]
    peer_count = lax.axis_size(TOA)
    per_peer = tile_count // peer_count
    owner_dev = owner_slot // tile_count
    owner_place = owner_slot % tile_count
    onehot_dest = (owner_dev[:, None] == jnp.arange(peer_count, dtype=jnp.int32)[None, :]).astype(
        jnp.int32
    )
    bucket_rank = jnp.sum((jnp.cumsum(onehot_dest, axis=0) - 1) * onehot_dest, axis=1)
    send_position = owner_dev * per_peer + bucket_rank
    send_order = (
        jnp.zeros((tile_count,), jnp.int32)
        .at[send_position]
        .set(jnp.arange(tile_count, dtype=jnp.int32))
    )
    onehot_pulsar, weight = tile_weights(
        residual, toa_error, pulsar, backend, counts, efac_table, equad_table
    )
    whitened_local = jnp.sqrt(weight) * residual
    place_float = owner_place[send_order][:, None].astype(jnp.float32)
    moved_white, moved_place = sent_together(
        (whitened_local[send_order], place_float), TOA, 0, 0, 1
    )
    whitened = jnp.zeros_like(moved_white).at[moved_place[:, 0].astype(jnp.int32)].set(moved_white)
    gram_matrix, projection = pulsar_terms(basis_rows, weight, residual, onehot_pulsar)
    return (gram_matrix, projection, whitened)


def solution(mesh):
    split = Mesh(
        mesh.devices.reshape(8, 4, 4, mesh.shape["rep"]), ("toa_0", "toa_1", "toa_2", "rep")
    )
    placed = (
        P(TOA, None),
        P(TOA, None),
        P(TOA, "rep", None),
        P(),
        P(),
        P(TOA),
        P(TOA),
        P(TOA),
        P(TOA),
    )
    return jax.shard_map(
        shards,
        mesh=split,
        in_specs=placed,
        out_specs=(P(TOA, None, "rep"), P(TOA, "rep"), P(TOA, None)),
        check_vma=False,
    )
```

profile of v0, /device:TPU:1, one launch (start us, length us, event | category | flops | bytes accessed | tf_op | source)
XLA Modules:
  0.0 153.0 jit_solution(5533874653531388217)
XLA Ops:
  7.3 0.7 all-gather.2.cloned.1.call-update
  8.0 0.3 fusion.10
  8.3 0.3 fusion.11
  8.6 1.6 %sqrt_multiply_fusion = (f32[128,256]{1,0:T(8,128)S(1)}, f32[128,256]{1,0:T(8,128)S(1)}) fusion(f32[128,256]{1,0:T(8,128)} %param.9, f32[128]{0:T(128)S(1)} %integer_pow.21, f32[128,256]{1,0:T(8,128)} %param.10, f32[128]{0:T(128)S(1)} %integer_pow.19, s32[128]{0:T(128)S(1)} %copy-done.3), kind=kLoop, calls=%fused_computation.21 | loop fusion | flops 229376 | bytes 525824 | tf_op jit(solution)/shard_map/mul | solution.py:120
  10.2 0.9 fusion.15
  11.2 1.9 %fusion.2 = f32[128,1,50]{2,1,0:T(1,128)S(1)} fusion(bf16[128,50,256]{2,0,1:T(8,128)(2,1)S(1)} %copy-done.1, bf16[128,256,1]{1,0,2:T(8,128)(2,1)S(1)} %fusion.15), kind=kOutput, calls=%fused_computation.7 | convolution fusion | flops 3276800 | bytes 3367936 | tf_op jit(solution)/shard_map/tjr,tr->tj/dot_general | solution.py:84
  13.1 0.3 fusion.18
  13.3 1.0 multiply_convert_fusion
  14.3 22.6 %all-gather.2.cloned.1.call-done = bf16[128,100,256]{2,0,1:T(8,128)(2,1)} async-done(((bf16[128,50,256]{2,0,1:T(8,128)(2,1)}), bf16[128,100,256]{2,0,1:T(8,128)(2,1)}) %all-gather.2.cloned.1.call-update) | async-done | bytes 6553616 | tf_op jit(solution)/shard_map/all_gather | solution.py:80
  36.9 10.3 %fusion.5 = f32[128,100,50]{1,2,0:T(8,128)} fusion(bf16[128,100,256]{2,0,1:T(8,128)(2,1)} %all-gather.2.cloned.1.call-done, bf16[128,50,256]{2,0,1:T(8,128)(2,1)S(1)} %multiply_convert_fusion), kind=kOutput, calls=%fused_computation.11 | convolution fusion | flops 327680000 | bytes 12390400 | tf_op jit(solution)/shard_map/tkr,tjr->tkj/dot_general | solution.py:78
  47.2 3.7 %copy.31 = f32[128,100,50]{0,2,1:T(8,128)S(1)} copy(f32[128,100,50]{1,2,0:T(8,128)} %fusion.5) | data formatting | bytes 5120000 | tf_op jit(solution)/shard_map/tkr,tjr->tkj/dot_general | solution.py:78
  50.8 1.7 %reshape.38 = f32[128,5000]{0,1:T(8,128)} reshape(f32[128,100,50]{0,2,1:T(8,128)S(1)} %copy.31) | data formatting | bytes 5120000 | tf_op jit(solution)/shard_map/reshape | solution.py:91
  52.5 4.0 %fusion.19 = f32[128,5000]{0,1:T(8,128)S(1)} fusion(f32[128,5000]{0,1:T(8,128)} %reshape.38, s32[128]{0:T(128)S(1)} %copy-done.4), kind=kOutput, calls=%fused_computation.32 | convolution fusion | flops 983056384 | bytes 5120512 | tf_op jit(solution)/shard_map/dot_general | solution.py:89
  56.5 1.7 %pad_maximum_fusion = f32[128,5050]{0,1:T(8,128)} fusion(f32[128,50]{0,1:T(8,128)S(1)} %fusion.18, f32[128,5000]{0,1:T(8,128)S(1)} %fusion.19), kind=kLoop, calls=%fused_computation.10 | loop fusion | flops 646400 | bytes 5171200 | tf_op jit(solution)/shard_map/concatenate | solution.py:30
  58.1 2.1 %copy.32 = f32[128,5050]{1,0:T(8,128)S(1)} copy(f32[128,5050]{0,1:T(8,128)} %pad_maximum_fusion) | data formatting | bytes 5171200 | tf_op jit(solution)/shard_map/concatenate | solution.py:30
  60.3 3.0 %copy.33 = f32[16,8,1,5050]{3,1,2,0:T(8,128)} copy(f32[16,8,1,5050]{3,0,1,2:T(8,128)S(1)} %bitcast.28) | data formatting | bytes 5171200 | tf_op jit(solution)/shard_map/transpose | solution.py:13
  63.3 6.4 %all-to-all-start = ((f32[16,8,1,5050]{3,1,2,0:T(8,128)}), f32[16,8,1,5050]{3,1,2,0:T(8,128)S(1)}, u32[]{:S(2)}, u32[]{:S(2)}) async-start(f32[16,8,1,5050]{3,1,2,0:T(8,128)} %copy.33), calls=%async_computation | async-start | bytes 5242880 | tf_op jit(solution)/shard_map/all_to_all | solution.py:18
  69.9 0.2 reduce_window_sum.11
  70.0 0.2 select_reduce_fusion
  70.2 1.0 scatter_custom_fusion
  71.2 1.2 gather_fusion.1
  72.6 0.8 gather_fusion
  73.4 0.9 copy.35
  74.2 35.6 %all-to-all-done = f32[16,8,1,5050]{3,1,2,0:T(8,128)S(1)} async-done(((f32[16,8,1,5050]{3,1,2,0:T(8,128)}), f32[16,8,1,5050]{3,1,2,0:T(8,128)S(1)}, u32[]{:S(2)}, u32[]{:S(2)}) %all-to-all-start) | async-done | bytes 2585632 | tf_op jit(solution)/shard_map/all_to_all | solution.py:18
  109.8 11.3 %all-to-all-start.2 = ((f32[128,1,257]{2,1,0:T(1,128)}), f32[128,1,257]{2,1,0:T(1,128)S(1)}, u32[]{:S(2)}, u32[]{:S(2)}) async-start(f32[128,1,257]{2,1,0:T(1,128)} %copy.35), calls=%async_computation.2 | async-start | bytes 393216 | tf_op jit(solution)/shard_map/all_to_all | solution.py:47
  121.2 0.8 reduce_sum.52
  122.0 11.0 %all-to-all-done.2 = f32[128,1,257]{2,1,0:T(1,128)S(1)} async-done(((f32[128,1,257]{2,1,0:T(1,128)}), f32[128,1,257]{2,1,0:T(1,128)S(1)}, u32[]{:S(2)}, u32[]{:S(2)}) %all-to-all-start.2) | async-done | bytes 131616 | tf_op jit(solution)/shard_map/all_to_all | solution.py:47
  133.0 3.4 %all-to-all-start.1 = ((f32[8,1,5050]{2,1,0:T(1,128)}), f32[8,1,5050]{2,1,0:T(1,128)S(1)}, u32[]{:S(2)}, u32[]{:S(2)}) async-start(f32[8,1,5050]{2,1,0:T(1,128)} %reduce_sum.52), calls=%async_computation.1 | async-start | bytes 327680 | tf_op jit(solution)/shard_map/all_to_all | solution.py:25
  136.5 1.6 %scatter_custom_fusion.1 = f32[128,256]{1,0:T(8,128)} fusion(s32[128]{0:T(128)S(1)} %fusion.24, f32[128,257]{1,0:T(8,128)S(1)} %bitcast.29, f32[]{:T(128)} %constant.37.clone.1), kind=kCustom, calls=%fused_computation.18 | custom fusion | bytes 262148 | tf_op jit(solution)/shard_map/scatter | solution.py:125
  138.2 6.4 %all-to-all-done.1 = f32[8,1,5050]{2,1,0:T(1,128)S(1)} async-done(((f32[8,1,5050]{2,1,0:T(1,128)}), f32[8,1,5050]{2,1,0:T(1,128)S(1)}, u32[]{:S(2)}, u32[]{:S(2)}) %all-to-all-start.1) | async-done | bytes 161632 | tf_op jit(solution)/shard_map/all_to_all | solution.py:25
  144.7 0.6 slice.13
  145.5 0.7 copy.38
  (35 shorter events, 0.9 us)
Async XLA Ops:
  7.2 0.8 copy-start
  7.2 4.0 %copy-start.1 = (bf16[128,50,256]{2,0,1:T(8,128)(2,1)S(1)}, bf16[128,50,256]{2,0,1:T(8,128)(2,1)}, u32[]{:S(2)}) copy-start(bf16[128,50,256]{2,0,1:T(8,128)(2,1)} %param.11) | copy-start | bytes 9830404
  7.2 0.8 copy-start.4
  7.2 0.8 copy-start.6
  7.2 1.1 copy-start.5
  7.2 1.4 copy-start.3
  7.2 29.6 %all-gather.2.cloned.1.call-start = ((), (), s32[]{:S(2)}) async-start(), calls=%async_computation.3 | async-start | bytes 9830400 | tf_op jit(solution)/shard_map/all_gather | solution.py:80
  8.0 5.3 %copy-start.2 = (bf16[128,50,256]{2,0,1:T(8,128)(2,1)S(1)}, bf16[128,50,256]{2,0,1:T(8,128)(2,1)}, u32[]{:S(2)}) copy-start(bf16[128,50,256]{2,0,1:T(8,128)(2,1)} %param.11) | copy-start | bytes 9830404
  63.3 6.4 %copy-start.7 = (s32[128]{0:T(128)S(1)}, s32[128]{0:T(128)}, u32[]{:S(2)}) copy-start(s32[128]{0:T(128)} %param.17) | copy-start | bytes 1540
  63.3 46.5 %all-to-all-start = ((f32[16,8,1,5050]{3,1,2,0:T(8,128)}), f32[16,8,1,5050]{3,1,2,0:T(8,128)S(1)}, u32[]{:S(2)}, u32[]{:S(2)}) async-start(f32[16,8,1,5050]{3,1,2,0:T(8,128)} %copy.33), calls=%async_computation | async-start | bytes 5242880 | tf_op jit(solution)/shard_map/all_to_all | solution.py:18
  109.8 23.1 %all-to-all-start.2 = ((f32[128,1,257]{2,1,0:T(1,128)}), f32[128,1,257]{2,1,0:T(1,128)S(1)}, u32[]{:S(2)}, u32[]{:S(2)}) async-start(f32[128,1,257]{2,1,0:T(1,128)} %copy.35), calls=%async_computation.2 | async-start | bytes 393216 | tf_op jit(solution)/shard_map/all_to_all | solution.py:47
  133.0 11.6 %all-to-all-start.1 = ((f32[8,1,5050]{2,1,0:T(1,128)}), f32[8,1,5050]{2,1,0:T(1,128)S(1)}, u32[]{:S(2)}, u32[]{:S(2)}) async-start(f32[8,1,5050]{2,1,0:T(1,128)} %reduce_sum.52), calls=%async_computation.1 | async-start | bytes 327680 | tf_op jit(solution)/shard_map/all_to_all | solution.py:25
Sparse Core Ops, SparseCore 0:
  9.8 26.9 all-gather.1
where the time goes:
time: 155 us; the launch traced here: 153 us
  waiting for transfers between devices  76.2 us (49%)
  starting transfers between devices  21.1 us (14%)
  local copies, waits for them, and re-layouts  18.5 us (12%)
  matrix products  17 us (11%)
  between operations  14.3 us (9%)
  other arithmetic  5.89 us (4%)
    all_to_all x1, waiting for transfers between devices, sum_at_owner(): lax.all_to_all(in_blocks(value, dim, peers), axis, 0, 0, tiled=True)  35.6 us
    all_gather x1, waiting for transfers between devices, pulsar_terms(): lax.all_gather(basis_own, 'rep', axis=1, tiled=True)  22.6 us
    all_to_all x1, starting transfers between devices, sent_together(): lax.all_to_all(both, axis, split_axis=split_dim, concat_axis=concat_dim,...  11.3 us
    all_to_all x1, waiting for transfers between devices, sent_together(): lax.all_to_all(both, axis, split_axis=split_dim, concat_axis=concat_dim,...  11 us
    dot_general x1, matrix products, pulsar_terms(): jnp.einsum('tkr,tjr->tkj', lax.all_gather(basis_own, 'rep', axis=1, tiled...  10.3 us
    all_to_all x1, waiting for transfers between devices, summed_rows(): return jnp.sum(lax.all_to_all(own, far, 0, 0, tiled=True), axis=0)  6.41 us
    all_to_all x1, starting transfers between devices, sum_at_owner(): lax.all_to_all(in_blocks(value, dim, peers), axis, 0, 0, tiled=True)  6.39 us
    dot_general x1, matrix products, pulsar_terms(): jnp.dot(onehot_pulsar.T, tile_gram.reshape(tile_total, full_width * half_...  4 us
  transfers between devices with their start and end apart: 4, of which 4 were waited for; matrix products, arithmetic and copies ran while one was open for 9% of the time, Pallas kernels for 0%

commit v1 on v0

v1 whole, which is shorter than its diff:
```python
import functools

import jax
import jax.numpy as jnp
from jax import lax
from jax.experimental import pallas as pl
from jax.experimental.pallas import tpu as pltpu
from jax.sharding import Mesh
from jax.sharding import PartitionSpec as P

TOA = ("toa_0", "toa_1", "toa_2")
FAR, NEAR = "toa_0", ("toa_1", "toa_2")
BF16, F32 = jnp.bfloat16, jnp.float32
LANES = 128
HALF = 64
GROUP = 16
HEAD = 24
WHITE = 32


def dot(a, b, **kw):
    return lax.dot_general(a, b, (((1,), (0,)), ((), ())), preferred_element_type=F32, **kw)


def iota(shape, dim):
    return lax.broadcasted_iota(jnp.int32, shape, dim)


def as_column(row, lanes):
    square = jnp.broadcast_to(row, (LANES, row.shape[1])).T
    return jnp.concatenate([square] * (lanes // LANES), axis=1)


def gram_kernel(
    near, far, pulsar_sm, residual, error, efac_t, equad_t, pulsar, backend, counts, slot,
    own, other, out, acc, weight_vm, wres_vm,
):
    cols, tiles, rows = own.shape
    message = out.shape[1]
    pulsars, backends = efac_t.shape[1], efac_t.shape[0]

    of_pulsar = (iota((pulsars, tiles), 0) == pulsar[...]).astype(F32)
    of_backend = (iota((backends, tiles), 0) == backend[...]).astype(F32)
    high = dict(precision=lax.Precision.HIGHEST)
    factor = jnp.sum(dot(efac_t[...], of_pulsar, **high) * of_backend, axis=0, keepdims=True)
    floor = jnp.sum(dot(equad_t[...], of_pulsar, **high) * of_backend, axis=0, keepdims=True)
    factor2 = as_column(factor * factor, rows)
    floor2 = as_column(floor * floor, rows)
    count = as_column(counts[...].astype(F32), rows)
    valid = iota((tiles, rows), 1).astype(F32) < count
    weight = jnp.where(valid, 1.0 / (factor2 * error[...] ** 2 + floor2), 0.0)
    weight_vm[...] = weight
    wres_vm[...] = (weight * residual[...]).astype(BF16)
    white = (jnp.sqrt(weight) * residual[...]).astype(BF16)

    dest = slot[...] // tiles
    place = (slot[...] % tiles).astype(F32)
    order = (dest % near) * far + dest // near
    moved = (iota((tiles, tiles), 0) == order).astype(BF16)
    white_to = dot(moved, white)
    place_to = dot(moved, as_column(place, LANES).astype(BF16))
    acc[...] = jnp.zeros_like(acc)
    for n in range(near):
        at = n * message
        acc[at : at + far, :] = white_to[n * far : (n + 1) * far, :LANES]
        acc[at + far : at + 2 * far, :] = white_to[n * far : (n + 1) * far, LANES:]
        acc[at + 2 * far : at + 3 * far, :] = place_to[n * far : (n + 1) * far, :]

    def turn(g, carry):
        t0 = pl.multiple_of(g * GROUP, GROUP)
        mine = own[:, pl.ds(t0, GROUP), :]
        extra = wres_vm[pl.ds(t0, GROUP), :].reshape(1, GROUP, rows)
        mine = pltpu.einshape("ktr->tkr", jnp.concatenate([mine, extra], axis=0))
        theirs = pltpu.einshape("ktr->tkr", other[:, pl.ds(t0, GROUP), :])
        group_weight = weight_vm[pl.ds(t0, GROUP), :]
        for u in range(GROUP):
            left = mine[u]
            wrow = group_weight[u : u + 1, :]
            scaled = (left.astype(F32) * wrow).astype(BF16)
            scaled = jnp.where(iota(left.shape, 0) < cols, scaled, left)
            right = lambda a: lax.dot_general(
                a, scaled, (((1,), (1,)), ((), ())), preferred_element_type=F32
            )
            p = pulsar_sm[t0 + u]
            base = (p % near) * message + HEAD + (p // near) * cols
            acc[pl.ds(base, cols), : cols + 1] += right(left)[:cols]
            acc[pl.ds(base, cols), HALF : HALF + cols + 1] += right(theirs[u])
        return carry

    lax.fori_loop(0, tiles // GROUP, turn, 0)

    def pack(n, carry):
        at = pl.multiple_of(n * message, 8)
        value = acc[pl.ds(at, message), :]
        rest = value - value.astype(BF16).astype(F32)
        rest = pltpu.roll(rest, 1, 1)
        lane, row = iota(value.shape, 1), iota(value.shape, 0)
        value = jnp.where((lane == cols + 1) & (row >= HEAD), rest, value)
        out[n] = value.astype(BF16)
        return carry

    lax.fori_loop(0, near, pack, 0)


def near_kernel(far, cols, got, out, total):
    near = got.shape[0]
    for half in range(2):
        part = got[:, half * far : (half + 1) * far, :].astype(F32)
        out[:, half * near : (half + 1) * near, :] = jnp.swapaxes(part, 0, 1).astype(BF16)
    place = jnp.zeros((far, LANES), F32)
    lane = iota((far, LANES), 1)
    summed = got[0, HEAD:, :].astype(F32)
    for n in range(near):
        place = jnp.where(lane == n, got[n, 2 * far : 3 * far, :].astype(F32), place)
        if n:
            summed = summed + got[n, HEAD:, :].astype(F32)
    total[: far * cols, :] = summed
    total[far * cols :, :] = place
    for f in range(far):
        out[f, WHITE : WHITE + cols, :] = total[f * cols : (f + 1) * cols, :].astype(BF16)
        out[f, WHITE + cols :, :] = jnp.broadcast_to(
            total[far * cols + f : far * cols + f + 1, :], (out.shape[1] - WHITE - cols, LANES)
        ).astype(BF16)


def far_kernel(cols, got, core, gram, proj, white):
    far, near = got.shape[0], WHITE // 2
    tiles = far * near
    place = jnp.zeros((1, LANES), F32)
    lane = iota((1, LANES), 1)
    total = jnp.zeros((got.shape[1] - WHITE, LANES), F32)
    for f in range(far):
        part = got[f, WHITE:, :].astype(F32)
        total = total + part
        row = part[cols : cols + 1, :]
        row = pltpu.roll(row, f * near, 1) if f else row
        place = jnp.where(lane // near == f, row, place)
    total = jnp.concatenate([total, jnp.zeros((LANES - total.shape[0], LANES), F32)], axis=0)
    turned = total.T
    mine = turned[:cols]
    theirs = turned[HALF : HALF + cols]
    first = core[0] == 0
    low = jnp.where(first, mine, theirs)
    high = jnp.where(first, theirs, mine)
    both = jnp.where(iota(low.shape, 1) < cols, low, pltpu.roll(high, cols, 1))
    gram[...] = both[:, : 2 * cols]
    proj[...] = (turned[cols : cols + 1] + turned[cols + 1 : cols + 2])[:, :cols]
    put = (iota((tiles, tiles), 0) == place.astype(jnp.int32)).astype(BF16)
    for half in range(2):
        rows = got[:, half * near : (half + 1) * near, :].reshape(tiles, LANES)
        white[:, half * LANES : (half + 1) * LANES] = dot(put, rows)


def vmem(n):
    return [pl.BlockSpec(memory_space=pltpu.VMEM)] * n


SMEM = pl.BlockSpec(memory_space=pltpu.SMEM)


def shards(
    residual, toa_error, basis_rows, efac_table, equad_table, pulsar, backend, counts, owner_slot
):
    far, near = lax.axis_size(FAR), lax.axis_size(NEAR)
    tiles, cols, rows = basis_rows.shape
    own = jnp.transpose(basis_rows, (1, 0, 2))
    other = lax.ppermute(own, "rep", [(0, 1), (1, 0)])
    message = HEAD + far * cols
    line = lambda a: a.reshape(1, -1)
    sent = pl.pallas_call(
        functools.partial(gram_kernel, near, far),
        out_shape=jax.ShapeDtypeStruct((near, message, LANES), BF16),
        in_specs=[SMEM] + vmem(10),
        out_specs=vmem(1)[0],
        scratch_shapes=[
            pltpu.VMEM((near * message, LANES), F32),
            pltpu.VMEM((tiles, rows), F32),
            pltpu.VMEM((tiles, rows), BF16),
        ],
        compiler_params=pltpu.CompilerParams(vmem_limit_bytes=40 << 20),
        name="gram",
    )(
        pulsar, residual, toa_error, efac_table.T, equad_table.T, line(pulsar), line(backend),
        line(counts), line(owner_slot), own, other,
    )
    got = lax.all_to_all(sent, NEAR, 0, 0, tiled=True)
    far_rows = WHITE + cols + 8 - (WHITE + cols) % 8
    sent = pl.pallas_call(
        functools.partial(near_kernel, far, cols),
        out_shape=jax.ShapeDtypeStruct((far, far_rows, LANES), BF16),
        in_specs=vmem(1),
        out_specs=vmem(1)[0],
        scratch_shapes=[pltpu.VMEM((far * cols + far, LANES), F32)],
        name="near_sum",
    )(got)
    got = lax.all_to_all(sent, FAR, 0, 0, tiled=True)
    core = lax.axis_index("rep").reshape(1)
    gram, projection, whitened = pl.pallas_call(
        functools.partial(far_kernel, cols),
        out_shape=(
            jax.ShapeDtypeStruct((cols, 2 * cols), F32),
            jax.ShapeDtypeStruct((1, cols), F32),
            jax.ShapeDtypeStruct((tiles, rows), F32),
        ),
        in_specs=vmem(1) + [SMEM],
        out_specs=tuple(vmem(3)),
        name="far_sum",
    )(got, core)
    return gram.T[None], projection, whitened


def solution(mesh):
    split = Mesh(
        mesh.devices.reshape(8, 4, 4, mesh.shape["rep"]), ("toa_0", "toa_1", "toa_2", "rep")
    )
    placed = (
        P(TOA, None),
        P(TOA, None),
        P(TOA, "rep", None),
        P(),
        P(),
        P(TOA),
        P(TOA),
        P(TOA),
        P(TOA),
    )
    return jax.shard_map(
        shards,
        mesh=split,
        in_specs=placed,
        out_specs=(P(TOA, None, "rep"), P(TOA, "rep"), P(TOA, None)),
        check_vma=False,
    )
```

time: 155 us -> 78.6 us (0.51)
  waiting for transfers between devices: 76.2 us -> 14.2 us
  blocking collectives: 0 us -> 29 us
  matrix products: 17 us -> 0 us
  between operations: 14.3 us -> 0.66 us
  Pallas kernels: 0 us -> 12.4 us
  starting transfers between devices: 21.1 us -> 11.5 us
  local copies, waits for them, and re-layouts: 18.5 us -> 9.92 us
  other arithmetic: 5.89 us -> 0 us
    all_to_all x3 -> x1, waiting for transfers between devices: 53 us -> 8.56 us  [shards(): got = lax.all_to_all(sent, FAR, 0, 0, tiled=True)]
    all_to_all x0 -> x1, blocking collectives: none -> 29 us  [shards(): got = lax.all_to_all(sent, NEAR, 0, 0, tiled=True)]
    all_gather x1 -> x0, waiting for transfers between devices: 22.6 us -> none  [pulsar_terms(): lax.all_gather(basis_own, 'rep', axis=1, tiled=True)]
    dot_general x6 -> x0, matrix products: 17 us -> none  [the longest x1 10.3 us: pulsar_terms(): jnp.einsum('tkr,tjr->tkj', lax.all_gather(basis_own, 'rep', axis=1, tiled...]
    all_to_all x3 -> x1, starting transfers between devices: 21 us -> 8.2 us  [shards(): got = lax.all_to_all(sent, FAR, 0, 0, tiled=True)]
    pallas_call x0 -> x3, Pallas kernels: none -> 12.4 us  [the longest x1 8.18 us: shards(): pl.pallas_call(functools.partial(gram_kernel, near, far), out_shape=jax.S...]
    unnamed x17 -> x21, local copies, waits for them, and re-layouts: 0.77 us -> 9.92 us
    ppermute x0 -> x1, waiting for transfers between devices: none -> 5.68 us  [shards(): other = lax.ppermute(own, 'rep', [(0, 1), (1, 0)])]
  transfers between devices with their start and end apart: 4 -> 2, of which waited for: 4 -> 2; matrix products, arithmetic and copies ran while one was open for 9% -> 0% of each run, Pallas kernels for 0% -> 0%
where the time goes in v1:
time: 78.6 us; the launch traced here: 77.7 us
  blocking collectives  29 us (37%)
  waiting for transfers between devices  14.2 us (18%)
  Pallas kernels  12.4 us (16%)
  starting transfers between devices  11.5 us (15%)
  local copies, waits for them, and re-layouts  9.92 us (13%)
    all_to_all x1, blocking collectives, shards(): got = lax.all_to_all(sent, NEAR, 0, 0, tiled=True)  29 us
    unnamed x21, local copies, waits for them, and re-layouts  9.92 us
    all_to_all x1, waiting for transfers between devices, shards(): got = lax.all_to_all(sent, FAR, 0, 0, tiled=True)  8.56 us
    all_to_all x1, starting transfers between devices, shards(): got = lax.all_to_all(sent, FAR, 0, 0, tiled=True)  8.2 us
    pallas_call x1, Pallas kernels, shards(): pl.pallas_call(functools.partial(gram_kernel, near, far), out_shape=jax.S...  8.18 us
    ppermute x1, waiting for transfers between devices, shards(): other = lax.ppermute(own, 'rep', [(0, 1), (1, 0)])  5.68 us
    ppermute x1, starting transfers between devices, shards(): other = lax.ppermute(own, 'rep', [(0, 1), (1, 0)])  3.29 us
    pallas_call x1, Pallas kernels, shards(): pl.pallas_call(functools.partial(near_kernel, far, cols), out_shape=jax.S...  2.44 us
  transfers between devices with their start and end apart: 2, of which 2 were waited for; matrix products, arithmetic and copies ran while one was open for 0% of the time, Pallas kernels for 0%

profile of v1, /device:TPU:1, one launch (start us, length us, event | category | flops | bytes accessed | tf_op | source)
XLA Modules:
  0.0 77.7 jit_solution(16446848060167966140)
XLA Ops:
  0.6 3.3 %collective-permute-start = (bf16[50,128,256]{2,1,0:T(8,128)(2,1)}, bf16[50,128,256]{2,1,0:T(8,128)(2,1)S(1)}, u32[]{:S(2)}, u32[]{:S(2)}) collective-permute-start(bf16[50,128,256]{2,1,0:T(8,128)(2,1)} %bitcast.11), channel_id=1, source_target_pairs={{0,1},{1,0},{2,3},{3,2},{4,5},{5,4},{6,7},{7,6},{8,9},{9,8},{10,11... | collective-permute-start | bytes 9830408 | tf_op jit(solution)/shard_map/ppermute | solution.py:167
  3.9 5.7 %collective-permute-done.other = bf16[50,128,256]{2,1,0:T(8,128)(2,1)S(1)} collective-permute-done((bf16[50,128,256]{2,1,0:T(8,128)(2,1)}, bf16[50,128,256]{2,1,0:T(8,128)(2,1)S(1)}, u32[]{:S(2)}, u32[]{:S(2)}) %collective-permute-start) | collective-permute-done | bytes 3276832 | tf_op jit(solution)/shard_map/ppermute | solution.py:167
  9.6 0.0 copy-start
  9.6 1.9 %copy-done = bf16[128,50,256]{2,0,1:T(8,128)(2,1)S(1)} copy-done((bf16[128,50,256]{2,0,1:T(8,128)(2,1)S(1)}, bf16[128,50,256]{2,0,1:T(8,128)(2,1)}, u32[]{:S(2)}) %copy-start) | copy-done | bytes 3276824
  11.5 0.0 copy-start.1
  11.5 0.9 %copy-done.1 = f32[128,256]{1,0:T(8,128)S(1)} copy-done((f32[128,256]{1,0:T(8,128)S(1)}, f32[128,256]{1,0:T(8,128)}, u32[]{:S(2)}) %copy-start.1) | copy-done | bytes 131096
  12.4 0.0 copy-start.2
  12.4 0.9 %copy-done.2 = f32[128,256]{1,0:T(8,128)S(1)} copy-done((f32[128,256]{1,0:T(8,128)S(1)}, f32[128,256]{1,0:T(8,128)}, u32[]{:S(2)}) %copy-start.2) | copy-done | bytes 131096
  13.3 0.0 copy-start.3
  13.3 0.8 copy-done.3
  14.1 0.0 copy-start.4
  14.1 0.8 copy-done.4
  14.9 0.0 copy-start.5
  14.9 0.7 copy-done.5
  15.5 0.0 copy-start.6
  15.5 0.7 copy-done.6
  16.2 0.0 copy-start.7
  16.2 0.7 copy-done.7
  16.8 0.0 copy-start.8
  16.8 0.7 copy-done.8
  17.5 8.2 %gram.1 = bf16[16,424,128]{2,1,0:T(8,128)(2,1)S(1)} custom-call(s32[128]{0:T(128)S(1)} %copy-done.5, f32[128,256]{1,0:T(8,128)S(1)} %copy-done.1, f32[128,256]{1,0:T(8,128)S(1)} %copy-done.2, f32[64,128]{1,0:T(8,128)S(1)} %bitcast.13, f32[64,128]{1,0:T(8,128)S(1)} %bitcast.14, s32[1,128]{1,0:T(1,128)S(1)} %bitcast.15, s32[1,128]{1,0:T(1,128)S(1)} %bitcast.16, ...), custom_call_target="tpu_custom_call" | custom-call | tf_op jit(solution)/shard_map/gram/pallas_call | solution.py:170
  25.7 29.0 %all_to_all.10.got = bf16[16,424,128]{2,1,0:T(8,128)(2,1)} all-to-all(bf16[16,424,128]{2,1,0:T(8,128)(2,1)S(1)} %gram.1), channel_id=1, replica_groups=mesh['toa_0'=8,'toa_1'=4,'toa_2'=4,'rep'=2] {'toa_1','toa_2'}, dimensions={0} | all-to-all | bytes 3473408 | tf_op jit(solution)/shard_map/all_to_all | solution.py:186
  54.6 2.4 %near_sum.1 = bf16[8,88,128]{2,1,0:T(8,128)(2,1)} custom-call(bf16[16,424,128]{2,1,0:T(8,128)(2,1)} %all_to_all.10.got), custom_call_target="tpu_custom_call" | custom-call | tf_op jit(solution)/shard_map/near_sum/pallas_call | solution.py:188
  57.1 8.2 %all-to-all-start.1 = ((bf16[8,88,128]{2,1,0:T(8,128)(2,1)}), bf16[8,88,128]{2,1,0:T(8,128)(2,1)S(1)}, u32[]{:S(2)}, u32[]{:S(2)}) async-start(bf16[8,88,128]{2,1,0:T(8,128)(2,1)} %near_sum.1), calls=%async_computation.1 | async-start | bytes 360448 | tf_op jit(solution)/shard_map/all_to_all | solution.py:196
  65.3 8.6 %all-to-all-done.1.got = bf16[8,88,128]{2,1,0:T(8,128)(2,1)S(1)} async-done(((bf16[8,88,128]{2,1,0:T(8,128)(2,1)}), bf16[8,88,128]{2,1,0:T(8,128)(2,1)S(1)}, u32[]{:S(2)}, u32[]{:S(2)}) %all-to-all-start.1) | async-done | bytes 180256 | tf_op jit(solution)/shard_map/all_to_all | solution.py:196
  73.8 0.0 copy-start.9
  73.8 0.7 copy-done.9
  74.5 1.8 %far_sum.1 = (f32[50,100]{1,0:T(8,128)}, f32[1,50]{1,0:T(1,128)}, f32[128,256]{1,0:T(8,128)}) custom-call(bf16[8,88,128]{2,1,0:T(8,128)(2,1)} %copy-done.9, s32[1]{0:T(128)} %bitcast.7.core), custom_call_target="tpu_custom_call" | custom-call | tf_op jit(solution)/shard_map/far_sum/pallas_call | solution.py:198
  76.3 1.4 %copy.12 = f32[1,100,50]{1,0,2:T(1,128)} copy(f32[1,100,50]{1,2,0:T(8,128)} %bitcast.19) | data formatting | bytes 40000
Async XLA Ops:
  0.6 9.0 %collective-permute-start = (bf16[50,128,256]{2,1,0:T(8,128)(2,1)}, bf16[50,128,256]{2,1,0:T(8,128)(2,1)S(1)}, u32[]{:S(2)}, u32[]{:S(2)}) collective-permute-start(bf16[50,128,256]{2,1,0:T(8,128)(2,1)} %bitcast.11), channel_id=1, source_target_pairs={{0,1},{1,0},{2,3},{3,2},{4,5},{5,4},{6,7},{7,6},{8,9},{9,8},{10,11... | collective-permute-start | bytes 9830408 | tf_op jit(solution)/shard_map/ppermute | solution.py:167
  9.6 1.9 %copy-start = (bf16[128,50,256]{2,0,1:T(8,128)(2,1)S(1)}, bf16[128,50,256]{2,0,1:T(8,128)(2,1)}, u32[]{:S(2)}) copy-start(bf16[128,50,256]{2,0,1:T(8,128)(2,1)} %param.11) | copy-start | bytes 9830404
  11.5 0.9 %copy-start.1 = (f32[128,256]{1,0:T(8,128)S(1)}, f32[128,256]{1,0:T(8,128)}, u32[]{:S(2)}) copy-start(f32[128,256]{1,0:T(8,128)} %residual.1) | copy-start | bytes 393220
  12.4 0.9 %copy-start.2 = (f32[128,256]{1,0:T(8,128)S(1)}, f32[128,256]{1,0:T(8,128)}, u32[]{:S(2)}) copy-start(f32[128,256]{1,0:T(8,128)} %error.1) | copy-start | bytes 393220
  13.3 0.8 copy-start.3
  14.1 0.8 copy-start.4
  14.9 0.7 copy-start.5
  15.5 0.7 copy-start.6
  16.2 0.7 copy-start.7
  16.8 0.7 copy-start.8
  57.1 16.8 %all-to-all-start.1 = ((bf16[8,88,128]{2,1,0:T(8,128)(2,1)}), bf16[8,88,128]{2,1,0:T(8,128)(2,1)S(1)}, u32[]{:S(2)}, u32[]{:S(2)}) async-start(bf16[8,88,128]{2,1,0:T(8,128)(2,1)} %near_sum.1), calls=%async_computation.1 | async-start | bytes 360448 | tf_op jit(solution)/shard_map/all_to_all | solution.py:196
  73.8 0.7 copy-start.9

commit v2 on v1

v2 whole, which is shorter than its diff:
```python
import functools

import jax
import jax.numpy as jnp
from jax import lax
from jax.experimental import pallas as pl
from jax.experimental.pallas import tpu as pltpu
from jax.sharding import Mesh
from jax.sharding import PartitionSpec as P

TOA = ("toa_0", "toa_1", "toa_2")
FAR, NEAR = "toa_0", ("toa_1", "toa_2")
BF16, F32 = jnp.bfloat16, jnp.float32
LANES = 128
GROUP = 16

PART = 25
WIDE = PART + 1
SECOND = 32
DIAGONAL = ((0, 7, 25), (7, 13, 58), (13, 25, 64))
CROSS = 76
PLACE = 126
WHITE = 32


def dot(a, b, dims=((1,), (0,)), **kw):
    return lax.dot_general(a, b, (dims, ((), ())), preferred_element_type=F32, **kw)


def iota(shape, dim):
    return lax.broadcasted_iota(jnp.int32, shape, dim)


def as_column(row, lanes):
    square = jnp.broadcast_to(row, (LANES, row.shape[1])).T
    return jnp.concatenate([square] * (lanes // LANES), axis=1)


def base_row(p, near, message, head):
    return (p % near) * message + head + (p // near) * WIDE


def own_kernel(
    near, far, pulsar_in, backend_in, counts_in, slot_in, residual_in, error_in, efac_in, equad_in,
    own_in, left_out, acc,
    pulsar, backend, counts, slot, residual, error, efac_t, equad_t, own, pulsar_sm,
    weight_vm, wres_vm, sems,
):
    cols, tiles, rows = own.shape
    head = 2 * far
    message = head + far * WIDE
    pulsars, backends = efac_t.shape[1], efac_t.shape[0]
    pairs = (
        (pulsar_in, pulsar), (backend_in, backend), (counts_in, counts), (slot_in, slot),
        (residual_in, residual), (error_in, error), (efac_in, efac_t), (equad_in, equad_t),
        (pulsar_in, pulsar_sm), (own_in, own),
    )
    copies = [pltpu.make_async_copy(a, b, sems.at[i]) for i, (a, b) in enumerate(pairs)]
    for copy in copies:
        copy.start()
    acc[...] = jnp.zeros_like(acc)
    for copy in copies[:-1]:
        copy.wait()

    of_pulsar = (iota((pulsars, tiles), 0) == pulsar[...]).astype(F32)
    of_backend = (iota((backends, tiles), 0) == backend[...]).astype(F32)
    high = dict(precision=lax.Precision.HIGHEST)
    factor = jnp.sum(dot(efac_t[...], of_pulsar, **high) * of_backend, axis=0, keepdims=True)
    floor = jnp.sum(dot(equad_t[...], of_pulsar, **high) * of_backend, axis=0, keepdims=True)
    factor2 = as_column(factor * factor, rows)
    floor2 = as_column(floor * floor, rows)
    count = as_column(counts[...].astype(F32), rows)
    valid = iota((tiles, rows), 1).astype(F32) < count
    weight = jnp.where(valid, 1.0 / (factor2 * error[...] ** 2 + floor2), 0.0)
    weight_vm[...] = weight
    wres_vm[...] = (weight * residual[...]).astype(BF16)
    white = (jnp.sqrt(weight) * residual[...]).astype(BF16)

    me = lax.axis_index("toa_1") * lax.axis_size("toa_2") + lax.axis_index("toa_2")
    dest = slot[...] // tiles
    place = (slot[...] % tiles).astype(F32)
    order = (dest % near) * far + dest // near
    moved = (iota((tiles, tiles), 0) == order).astype(BF16)
    white_to = dot(moved, white)
    place_to = dot(moved, as_column(place, LANES).astype(BF16))
    place_to = jnp.where(iota(place_to.shape, 1) == PLACE, place_to, 0.0)
    for n in range(near):
        at = n * message
        acc[at : at + far, :] = white_to[n * far : (n + 1) * far, :LANES]
        acc[at + far : at + 2 * far, :] = white_to[n * far : (n + 1) * far, LANES:]
        acc[pl.ds(at + head + me, far, stride=WIDE), :] = place_to[n * far : (n + 1) * far, :]
    copies[-1].wait()

    lefts = 2 * SECOND
    wide = 80
    lane, row = iota((SECOND, wide), 1), iota((SECOND, wide), 0)
    own_lane = (lane < PART) | ((lane >= SECOND) & (lane < SECOND + PART))
    second = (~own_lane) | (row == PART)
    kept = own_lane | (row != PART)
    is_wres = iota((lefts, rows), 0) == SECOND + PART

    def turn(g, carry):
        t0 = pl.multiple_of(g * GROUP, GROUP)
        here = pl.ds(t0, GROUP)
        slabs = [
            own[:PART, here, :],
            own[PART : PART + 7, here, :],
            own[PART:, here, :],
            wres_vm[here, :].reshape(1, GROUP, rows),
            own[PART + 7 : PART + 13, here, :],
            own[PART + 13 :, here, :],
            jnp.zeros((4, GROUP, rows), BF16),
        ]
        turned = pltpu.einshape("ktr->tkr", jnp.concatenate(slabs, axis=0))
        group_weight = weight_vm[here, :]
        for u in range(GROUP):
            left = turned[u][:lefts]
            scaled = (left.astype(F32) * group_weight[u : u + 1, :]).astype(BF16)
            scaled = jnp.where(is_wres, left, scaled)
            left_out[t0 + u] = scaled
            out = dot(scaled, turned[u], ((1,), (1,)))
            value = jnp.where(kept, jnp.where(second, out[SECOND:], out[:SECOND]), 0.0)
            base = base_row(pulsar_sm[0, t0 + u], near, message, head)
            acc[pl.ds(base, WIDE), :wide] += value[:WIDE]
        return carry

    lax.fori_loop(0, tiles // GROUP, turn, 0)


def cross_kernel(near, far, pulsar_sm, left, acc_own, other, out, acc):
    cols, tiles, rows = other.shape
    head = 2 * far
    message = head + far * WIDE
    core = lax.axis_index("rep")
    acc[...] = jnp.zeros_like(acc)
    second = iota((SECOND, cols), 1) >= PART

    def turn(g, carry):
        t0 = pl.multiple_of(g * GROUP, GROUP)
        here = pl.ds(t0, GROUP)
        slabs = [other[pl.ds(PART * core, PART), here, :], other[pl.ds(PART - PART * core, PART), here, :]]
        turned = pltpu.einshape("ktr->tkr", jnp.concatenate(slabs, axis=0))
        for u in range(GROUP):
            product = dot(left[t0 + u], turned[u], ((1,), (1,)))
            value = jnp.where(second, product[SECOND:], product[:SECOND])
            base = base_row(pulsar_sm[0, t0 + u], near, message, head)
            acc[pl.ds(base, PART), :cols] += value[:PART]
        return carry

    lax.fori_loop(0, tiles // GROUP, turn, 0)

    lane, row = iota((message, LANES), 1), iota((message, LANES), 0) - head
    rest_here = (row >= 0) & (row % WIDE == PART) & (lane >= LANES // 2)

    def pack(n, carry):
        here = pl.ds(pl.multiple_of(n * message, 8), message)
        value = acc_own[here, :] + pltpu.roll(acc[here, :], CROSS, 1)
        rest = pltpu.roll(value - value.astype(BF16).astype(F32), LANES // 2, 1)
        out[n] = jnp.where(rest_here, rest, value).astype(BF16)
        return carry

    lax.fori_loop(0, near, pack, 0)


def near_kernel(far, got, out, total):
    near = got.shape[0]
    head = 2 * far
    for half in range(2):
        part = got[:, half * far : (half + 1) * far, :].astype(F32)
        out[:, half * near : (half + 1) * near, :] = jnp.swapaxes(part, 0, 1).astype(BF16)
    summed = got[0, head:, :].astype(F32)
    for n in range(1, near):
        summed = summed + got[n, head:, :].astype(F32)
    total[: far * WIDE, :] = summed
    total[far * WIDE :, :] = jnp.zeros((total.shape[0] - far * WIDE, LANES), F32)
    lane, row = iota((SECOND, LANES), 1), iota((SECOND, LANES), 0)
    for f in range(far):
        block = total[f * WIDE : f * WIDE + SECOND, :]
        joined = block + pltpu.roll(block, LANES // 2, 1)
        rest = joined - joined.astype(BF16).astype(F32)
        split = jnp.where(lane < LANES // 2, joined, rest)
        out[f, WHITE:, :] = jnp.where(row == PART, split, block).astype(BF16)


def far_kernel(got, out):
    total = got[0, WHITE:, :].astype(F32)
    for f in range(1, got.shape[0]):
        total = total + got[f, WHITE:, :].astype(F32)
    out[...] = total


def white_kernel(got, white):
    far, near = got.shape[0], WHITE // 2
    tiles = far * near
    lane = iota((near, LANES), 1)
    puts = []
    for f in range(far):
        value = got[f, WHITE : WHITE + near, :].astype(F32)
        place = jnp.sum(jnp.where(lane == PLACE, value, 0.0), axis=1, keepdims=True)
        puts.append((lane.astype(F32) == place).astype(F32))
    put = jnp.concatenate(puts, axis=0).astype(BF16)
    for half in range(2):
        rows = got[:, half * near : (half + 1) * near, :].reshape(tiles, LANES)
        white[:, half * LANES : (half + 1) * LANES] = dot(put, rows, ((0,), (0,)))


def join_kernel(mine_in, theirs_in, gram, proj):
    mine, theirs = mine_in[...], theirs_in[...]
    lane = iota((SECOND, LANES), 1)

    def square(a):
        return jnp.concatenate([a, jnp.zeros((LANES - SECOND, LANES), F32)], axis=0).T

    cross = pltpu.roll(mine, LANES - CROSS, 1)
    turned = square(mine)[SECOND : 2 * SECOND]
    theirs_t = square(pltpu.roll(theirs, LANES - CROSS, 1))
    theirs_0 = theirs_t[:SECOND]
    theirs_1 = theirs_t[PART : PART + SECOND]

    def laid(pieces):
        value = jnp.zeros((SECOND, LANES), F32)
        for source, start, width, to in pieces:
            moved = pltpu.roll(source, (to - start) % LANES, 1) if to != start else source
            value = jnp.where((lane >= to) & (lane < to + width), moved, value)
        return value

    def write(own, cross_at):
        low, high = cross_at
        top = [(mine, 0, PART, own), (mine, SECOND, PART, own + PART)]
        under = [(turned, 0, PART, own)]
        under += [(mine, at, b - a, own + PART + a) for a, b, at in DIAGONAL]
        if own == 0:
            top += [(cross, 0, PART, low), (theirs_1, 0, PART, high)]
            under += [(theirs_0, 0, PART, low), (cross, PART, PART, high)]
        else:
            top += [(theirs_0, 0, PART, low), (cross, 0, PART, high)]
            under += [(cross, PART, PART, low), (theirs_1, 0, PART, high)]
        gram[:PART, :] = laid(top)[:PART, : 4 * PART]
        gram[PART:, :] = laid(under)[:PART, : 4 * PART]

    core = lax.axis_index("rep")

    @pl.when(core == 0)
    def _():
        write(0, (2 * PART, 3 * PART))

    @pl.when(core == 1)
    def _():
        write(2 * PART, (0, PART))

    sums = mine + pltpu.roll(mine, LANES // 2, 1)
    proj[...] = laid([(sums, 0, PART, 0), (sums, SECOND, PART, PART)])[PART:WIDE, : 2 * PART]


def vmem(n):
    return [pl.BlockSpec(memory_space=pltpu.VMEM)] * n


SMEM = pl.BlockSpec(memory_space=pltpu.SMEM)
ANY = pl.BlockSpec(memory_space=pl.ANY)
SWAP = [(0, 1), (1, 0)]


def shards(
    residual, toa_error, basis_rows, efac_table, equad_table, pulsar, backend, counts, owner_slot
):
    far, near = lax.axis_size(FAR), lax.axis_size(NEAR)
    tiles, cols, rows = basis_rows.shape
    own = jnp.transpose(basis_rows, (1, 0, 2))
    other = lax.ppermute(own, "rep", SWAP)
    message = 2 * far + far * WIDE
    line = lambda a: a.reshape(1, -1)
    ints = [line(a) for a in (pulsar, backend, counts, owner_slot)]
    left, acc = pl.pallas_call(
        functools.partial(own_kernel, near, far),
        out_shape=(
            jax.ShapeDtypeStruct((tiles, 2 * SECOND, rows), BF16),
            jax.ShapeDtypeStruct((near * message, LANES), F32),
        ),
        in_specs=[ANY] * 9,
        out_specs=tuple(vmem(2)),
        scratch_shapes=[pltpu.VMEM((1, tiles), jnp.int32)] * 4
        + [pltpu.VMEM((tiles, rows), F32)] * 2
        + [pltpu.VMEM(efac_table.shape[::-1], F32)] * 2
        + [
            pltpu.VMEM(own.shape, BF16),
            pltpu.SMEM((1, tiles), jnp.int32),
            pltpu.VMEM((tiles, rows), F32),
            pltpu.VMEM((tiles, rows), BF16),
            pltpu.SemaphoreType.DMA((10,)),
        ],
        compiler_params=pltpu.CompilerParams(vmem_limit_bytes=32 << 20),
        cost_estimate=pl.CostEstimate(flops=2 * 10**9, transcendentals=0, bytes_accessed=10**7),
        name="own",
    )(*ints, residual, toa_error, efac_table.T, equad_table.T, own)
    sent = pl.pallas_call(
        functools.partial(cross_kernel, near, far),
        out_shape=jax.ShapeDtypeStruct((near, message, LANES), BF16),
        in_specs=[SMEM] + vmem(3),
        out_specs=vmem(1)[0],
        scratch_shapes=[pltpu.VMEM((near * message, LANES), F32)],
        compiler_params=pltpu.CompilerParams(vmem_limit_bytes=32 << 20),
        name="cross",
    )(ints[0], left, acc, other)
    got = lax.all_to_all(sent, NEAR, 0, 0, tiled=True)
    sent = pl.pallas_call(
        functools.partial(near_kernel, far),
        out_shape=jax.ShapeDtypeStruct((far, WHITE + SECOND, LANES), BF16),
        in_specs=vmem(1),
        out_specs=vmem(1)[0],
        scratch_shapes=[pltpu.VMEM((far * WIDE + 8, LANES), F32)],
        name="near_sum",
    )(got)
    got = lax.all_to_all(sent, FAR, 0, 0, tiled=True)
    mine = pl.pallas_call(
        far_kernel,
        out_shape=jax.ShapeDtypeStruct((SECOND, LANES), F32),
        in_specs=vmem(1),
        out_specs=vmem(1)[0],
        name="far_sum",
    )(got)
    theirs = lax.ppermute(mine, "rep", SWAP)
    whitened = pl.pallas_call(
        white_kernel,
        out_shape=jax.ShapeDtypeStruct((tiles, rows), F32),
        in_specs=vmem(1),
        out_specs=vmem(1)[0],
        cost_estimate=pl.CostEstimate(flops=10**7, transcendentals=0, bytes_accessed=10**6),
        name="white",
    )(got)
    gram, projection = pl.pallas_call(
        join_kernel,
        out_shape=(
            jax.ShapeDtypeStruct((cols, 2 * cols), F32),
            jax.ShapeDtypeStruct((1, cols), F32),
        ),
        in_specs=vmem(2),
        out_specs=tuple(vmem(2)),
        name="join",
    )(mine, theirs)
    return gram.T[None], projection, whitened


def solution(mesh):
    split = Mesh(
        mesh.devices.reshape(8, 4, 4, mesh.shape["rep"]), ("toa_0", "toa_1", "toa_2", "rep")
    )
    placed = (
        P(TOA, None),
        P(TOA, None),
        P(TOA, "rep", None),
        P(),
        P(),
        P(TOA),
        P(TOA),
        P(TOA),
        P(TOA),
    )
    return jax.shard_map(
        shards,
        mesh=split,
        in_specs=placed,
        out_specs=(P(TOA, None, "rep"), P(TOA, "rep"), P(TOA, None)),
        check_vma=False,
    )
```

time: 78.6 us -> 72.2 us (0.919)
  waiting for transfers between devices: 14.2 us -> 0.01 us
  blocking collectives: 29 us -> 36.4 us
  Pallas kernels: 12.4 us -> 18.4 us
  starting transfers between devices: 11.5 us -> 6.15 us
    all_to_all x0 -> x1, blocking collectives: none -> 16.2 us  [shards(): got = lax.all_to_all(sent, FAR, 0, 0, tiled=True)]
    all_to_all x1, blocking collectives: 29 us -> 20.2 us  [shards(): got = lax.all_to_all(sent, NEAR, 0, 0, tiled=True)]
    all_to_all x1 -> x0, waiting for transfers between devices: 8.56 us -> none  [shards(): got = lax.all_to_all(sent, FAR, 0, 0, tiled=True)]
    all_to_all x1 -> x0, starting transfers between devices: 8.2 us -> none  [shards(): got = lax.all_to_all(sent, FAR, 0, 0, tiled=True)]
    pallas_call x3 -> x6, Pallas kernels: 12.4 us -> 18.4 us  [the longest x1 6.04 us: shards(): pl.pallas_call(functools.partial(cross_kernel, near, far), out_shape=jax....]
    ppermute x1 -> x2, waiting for transfers between devices: 5.68 us -> 0.01 us  [the longest x1 0.01 us: shards(): other = lax.ppermute(own, 'rep', SWAP)]
    ppermute x1 -> x2, starting transfers between devices: 3.29 us -> 6.15 us  [the longest x1 3.29 us: shards(): other = lax.ppermute(own, 'rep', SWAP)]
  transfers between devices with their start and end apart: 2 -> 2, of which waited for: 2 -> 0; matrix products, arithmetic and copies ran while one was open for 0% -> 0% of each run, Pallas kernels for 0% -> 10%
where the time goes in v2:
time: 72.2 us; the launch traced here: 71.5 us
  blocking collectives  36.4 us (50%)
  Pallas kernels  18.4 us (25%)
  local copies, waits for them, and re-layouts  9.85 us (14%)
  starting transfers between devices  6.15 us (9%)
    all_to_all x1, blocking collectives, shards(): got = lax.all_to_all(sent, NEAR, 0, 0, tiled=True)  20.2 us
    all_to_all x1, blocking collectives, shards(): got = lax.all_to_all(sent, FAR, 0, 0, tiled=True)  16.2 us
    unnamed x21, local copies, waits for them, and re-layouts  9.85 us
    pallas_call x1, Pallas kernels, shards(): pl.pallas_call(functools.partial(cross_kernel, near, far), out_shape=jax....  6.04 us
    pallas_call x1, Pallas kernels, shards(): pl.pallas_call(functools.partial(own_kernel, near, far), out_shape=(jax.S...  5.34 us
    ppermute x1, starting transfers between devices, shards(): other = lax.ppermute(own, 'rep', SWAP)  3.29 us
    ppermute x1, starting transfers between devices, shards(): theirs = lax.ppermute(mine, 'rep', SWAP)  2.87 us
    pallas_call x1, Pallas kernels, shards(): pl.pallas_call(functools.partial(near_kernel, far), out_shape=jax.ShapeDt...  2.04 us
  transfers between devices with their start and end apart: 2, of which 0 were waited for; matrix products, arithmetic and copies ran while one was open for 0% of the time, Pallas kernels for 10%

profile of v2, /device:TPU:1, one launch (start us, length us, event | category | flops | bytes accessed | tf_op | source)
XLA Modules:
  0.0 71.5 jit_solution(6832138245742160583)
XLA Ops:
  0.6 3.3 %collective-permute-start = (bf16[50,128,256]{2,1,0:T(8,128)(2,1)}, bf16[50,128,256]{2,1,0:T(8,128)(2,1)S(1)}, u32[]{:S(2)}, u32[]{:S(2)}) collective-permute-start(bf16[50,128,256]{2,1,0:T(8,128)(2,1)} %bitcast.12), channel_id=1, source_target_pairs={{0,1},{1,0},{2,3},{3,2},{4,5},{5,4},{6,7},{7,6},{8,9},{9,8},{10,11... | collective-permute-start | bytes 9830408 | tf_op jit(solution)/shard_map/ppermute | solution.py:270
  3.9 0.0 copy-start
  3.9 0.7 copy-done
  4.6 0.0 copy-start.1
  4.6 1.9 %copy-done.1 = bf16[128,50,256]{2,0,1:T(8,128)(2,1)S(1)} copy-done((bf16[128,50,256]{2,0,1:T(8,128)(2,1)S(1)}, bf16[128,50,256]{2,0,1:T(8,128)(2,1)}, u32[]{:S(2)}) %copy-start.1) | copy-done | bytes 3276824
  6.5 0.0 copy-start.2
  6.5 0.9 %copy-done.2 = f32[128,256]{1,0:T(8,128)S(1)} copy-done((f32[128,256]{1,0:T(8,128)S(1)}, f32[128,256]{1,0:T(8,128)}, u32[]{:S(2)}) %copy-start.2) | copy-done | bytes 131096
  7.4 0.0 copy-start.3
  7.4 0.9 %copy-done.3 = f32[128,256]{1,0:T(8,128)S(1)} copy-done((f32[128,256]{1,0:T(8,128)S(1)}, f32[128,256]{1,0:T(8,128)}, u32[]{:S(2)}) %copy-start.3) | copy-done | bytes 131096
  8.3 0.0 copy-start.4
  8.3 0.8 %copy-done.4 = f32[128,64]{0,1:T(8,128)S(1)} copy-done((f32[128,64]{0,1:T(8,128)S(1)}, f32[128,64]{0,1:T(8,128)}, u32[]{:S(2)}) %copy-start.4) | copy-done | bytes 32792
  9.1 0.0 copy-start.5
  9.1 0.8 %copy-done.5 = f32[128,64]{0,1:T(8,128)S(1)} copy-done((f32[128,64]{0,1:T(8,128)S(1)}, f32[128,64]{0,1:T(8,128)}, u32[]{:S(2)}) %copy-start.5) | copy-done | bytes 32792
  9.8 0.7 copy-done.6
  10.5 0.0 copy-start.7
  10.5 0.7 copy-done.7
  11.1 0.0 copy-start.8
  11.1 0.7 copy-done.8
  11.8 5.3 %own.1 = (bf16[128,64,256]{2,1,0:T(8,128)(2,1)S(1)}, f32[3584,128]{1,0:T(8,128)S(1)}) custom-call(s32[1,128]{1,0:T(1,128)S(1)} %bitcast.10, s32[1,128]{1,0:T(1,128)S(1)} %bitcast.16, s32[1,128]{1,0:T(1,128)S(1)} %bitcast.17, s32[1,128]{1,0:T(1,128)S(1)} %bitcast.18, f32[128,256]{1,0:T(8,128)S(1)} %copy-done.2, f32[128,256]{1,0:T(8,128)S(1)} %copy-done.3, ...), custom_call_target="tpu_custom_call" | custom-call | flops 2000000000 | bytes 10000000 | tf_op jit(solution)/shard_map/own/pallas_call | solution.py:274
  17.1 0.0 collective-permute-done.other
  17.2 6.0 %cross.1 = bf16[16,224,128]{2,1,0:T(8,128)(2,1)S(1)} custom-call(s32[1,128]{1,0:T(1,128)S(1)} %bitcast.11, bf16[128,64,256]{2,1,0:T(8,128)(2,1)S(1)} %get-tuple-element.7.left, f32[3584,128]{1,0:T(8,128)S(1)} %get-tuple-element.8.acc_own, bf16[50,128,256]{2,1,0:T(8,128)(2,1)S(1)} %collective-permute-done.other), custom_call_target="tpu_custom_call" | custom-call | tf_op jit(solution)/shard_map/cross/pallas_call | solution.py:296
  23.2 20.2 %all_to_all.10.got = bf16[16,224,128]{2,1,0:T(8,128)(2,1)} all-to-all(bf16[16,224,128]{2,1,0:T(8,128)(2,1)S(1)} %cross.1), channel_id=1, replica_groups=mesh['toa_0'=8,'toa_1'=4,'toa_2'=4,'rep'=2] {'toa_1','toa_2'}, dimensions={0} | all-to-all | bytes 1835008 | tf_op jit(solution)/shard_map/all_to_all | solution.py:305
  43.4 2.0 %near_sum.1 = bf16[8,64,128]{2,1,0:T(8,128)(2,1)} custom-call(bf16[16,224,128]{2,1,0:T(8,128)(2,1)} %all_to_all.10.got), custom_call_target="tpu_custom_call" | custom-call | tf_op jit(solution)/shard_map/near_sum/pallas_call | solution.py:306
  45.5 16.2 %all_to_all.11.got = bf16[8,64,128]{2,1,0:T(8,128)(2,1)} all-to-all(bf16[8,64,128]{2,1,0:T(8,128)(2,1)} %near_sum.1), channel_id=1, replica_groups=mesh['toa_0'=8,'toa_1'=4,'toa_2'=4,'rep'=2] {'toa_0'}, dimensions={0} | all-to-all | bytes 262144 | tf_op jit(solution)/shard_map/all_to_all | solution.py:314
  61.7 1.5 %far_sum.1.mine_in = f32[32,128]{1,0:T(8,128)} custom-call(bf16[8,64,128]{2,1,0:T(8,128)(2,1)} %all_to_all.11.got), custom_call_target="tpu_custom_call" | custom-call | tf_op jit(solution)/shard_map/far_sum/pallas_call | solution.py:315
  63.2 2.9 %collective-permute-start.1 = (f32[32,128]{1,0:T(8,128)}, f32[32,128]{1,0:T(8,128)S(1)}, u32[]{:S(2)}, u32[]{:S(2)}) collective-permute-start(f32[32,128]{1,0:T(8,128)} %far_sum.1.mine_in), channel_id=1, source_target_pairs={{0,1},{1,0},{2,3},{3,2},{4,5},{5,4},{6,7},{7,6},{8,9},{9,8},{10,11... | collective-permute-start | bytes 49160 | tf_op jit(solution)/shard_map/ppermute | solution.py:322
  66.1 1.8 %white.1 = f32[128,256]{1,0:T(8,128)} custom-call(bf16[8,64,128]{2,1,0:T(8,128)(2,1)} %all_to_all.11.got), custom_call_target="tpu_custom_call" | custom-call | flops 10000000 | bytes 1000000 | tf_op jit(solution)/shard_map/white/pallas_call | solution.py:323
  67.9 0.0 collective-permute-done.1.theirs_in
  67.9 0.0 copy-start.9
  67.9 0.6 copy-done.9
  68.5 1.6 %join.1 = (f32[50,100]{1,0:T(8,128)}, f32[1,50]{1,0:T(1,128)}) custom-call(f32[32,128]{1,0:T(8,128)} %far_sum.1.mine_in, f32[32,128]{1,0:T(8,128)} %copy-done.9), custom_call_target="tpu_custom_call" | custom-call | tf_op jit(solution)/shard_map/join/pallas_call | solution.py:331
  70.1 1.4 %copy.12 = f32[1,100,50]{1,0,2:T(1,128)} copy(f32[1,100,50]{1,2,0:T(8,128)} %bitcast.19) | data formatting | bytes 40000
  (1 shorter events, 0.0 us)
Async XLA Ops:
  0.6 16.5 %collective-permute-start = (bf16[50,128,256]{2,1,0:T(8,128)(2,1)}, bf16[50,128,256]{2,1,0:T(8,128)(2,1)S(1)}, u32[]{:S(2)}, u32[]{:S(2)}) collective-permute-start(bf16[50,128,256]{2,1,0:T(8,128)(2,1)} %bitcast.12), channel_id=1, source_target_pairs={{0,1},{1,0},{2,3},{3,2},{4,5},{5,4},{6,7},{7,6},{8,9},{9,8},{10,11... | collective-permute-start | bytes 9830408 | tf_op jit(solution)/shard_map/ppermute | solution.py:270
  3.9 0.7 copy-start
  4.6 1.9 %copy-start.1 = (bf16[128,50,256]{2,0,1:T(8,128)(2,1)S(1)}, bf16[128,50,256]{2,0,1:T(8,128)(2,1)}, u32[]{:S(2)}) copy-start(bf16[128,50,256]{2,0,1:T(8,128)(2,1)} %param.11) | copy-start | bytes 9830404
  6.5 0.9 %copy-start.2 = (f32[128,256]{1,0:T(8,128)S(1)}, f32[128,256]{1,0:T(8,128)}, u32[]{:S(2)}) copy-start(f32[128,256]{1,0:T(8,128)} %residual_in.1) | copy-start | bytes 393220
  7.4 0.9 %copy-start.3 = (f32[128,256]{1,0:T(8,128)S(1)}, f32[128,256]{1,0:T(8,128)}, u32[]{:S(2)}) copy-start(f32[128,256]{1,0:T(8,128)} %error_in.1) | copy-start | bytes 393220
  8.3 0.8 %copy-start.4 = (f32[128,64]{0,1:T(8,128)S(1)}, f32[128,64]{0,1:T(8,128)}, u32[]{:S(2)}) copy-start(f32[128,64]{0,1:T(8,128)} %param.12) | copy-start | bytes 98308
  9.1 0.8 %copy-start.5 = (f32[128,64]{0,1:T(8,128)S(1)}, f32[128,64]{0,1:T(8,128)}, u32[]{:S(2)}) copy-start(f32[128,64]{0,1:T(8,128)} %param.13) | copy-start | bytes 98308
  9.8 0.7 copy-start.6
  10.5 0.7 copy-start.7
  11.1 0.7 copy-start.8
  63.2 4.7 %collective-permute-start.1 = (f32[32,128]{1,0:T(8,128)}, f32[32,128]{1,0:T(8,128)S(1)}, u32[]{:S(2)}, u32[]{:S(2)}) collective-permute-start(f32[32,128]{1,0:T(8,128)} %far_sum.1.mine_in), channel_id=1, source_target_pairs={{0,1},{1,0},{2,3},{3,2},{4,5},{5,4},{6,7},{7,6},{8,9},{9,8},{10,11... | collective-permute-start | bytes 49160 | tf_op jit(solution)/shard_map/ppermute | solution.py:322
  67.9 0.6 copy-start.9

commit v3 on v2

--- a/solution.py
+++ b/solution.py
@@ -235,8 +235,8 @@
         else:
             top += [(theirs_0, 0, PART, low), (cross, 0, PART, high)]
             under += [(cross, PART, PART, low), (theirs_1, 0, PART, high)]
-        gram[:PART, :] = laid(top)[:PART, : 4 * PART]
-        gram[PART:, :] = laid(under)[:PART, : 4 * PART]
+        gram[:PART, 0, :] = laid(top)[:PART, : 4 * PART]
+        gram[PART:, 0, :] = laid(under)[:PART, : 4 * PART]
 
     core = lax.axis_index("rep")
 
@@ -257,8 +257,16 @@
 
 
 SMEM = pl.BlockSpec(memory_space=pltpu.SMEM)
-ANY = pl.BlockSpec(memory_space=pl.ANY)
+HBM = pl.BlockSpec(memory_space=pltpu.HBM)
 SWAP = [(0, 1), (1, 0)]
+
+
+def stay(a):
+    return pltpu.with_memory_space_constraint(a, pltpu.HBM)
+
+
+def near_by(a):
+    return pltpu.with_memory_space_constraint(a, pltpu.VMEM)
 
 
 def shards(
@@ -277,7 +285,7 @@
             jax.ShapeDtypeStruct((tiles, 2 * SECOND, rows), BF16),
             jax.ShapeDtypeStruct((near * message, LANES), F32),
         ),
-        in_specs=[ANY] * 9,
+        in_specs=[HBM] * 9,
         out_specs=tuple(vmem(2)),
         scratch_shapes=[pltpu.VMEM((1, tiles), jnp.int32)] * 4
         + [pltpu.VMEM((tiles, rows), F32)] * 2
@@ -292,7 +300,7 @@
         compiler_params=pltpu.CompilerParams(vmem_limit_bytes=32 << 20),
         cost_estimate=pl.CostEstimate(flops=2 * 10**9, transcendentals=0, bytes_accessed=10**7),
         name="own",
-    )(*ints, residual, toa_error, efac_table.T, equad_table.T, own)
+    )(*map(stay, (*ints, residual, toa_error, efac_table.T, equad_table.T, own)))
     sent = pl.pallas_call(
         functools.partial(cross_kernel, near, far),
         out_shape=jax.ShapeDtypeStruct((near, message, LANES), BF16),
@@ -305,20 +313,20 @@
     got = lax.all_to_all(sent, NEAR, 0, 0, tiled=True)
     sent = pl.pallas_call(
         functools.partial(near_kernel, far),
-        out_shape=jax.ShapeDtypeStruct((far, WHITE + SECOND, LANES), BF16),
+        out_shape=pltpu.VMEM((far, WHITE + SECOND, LANES), BF16),
         in_specs=vmem(1),
         out_specs=vmem(1)[0],
         scratch_shapes=[pltpu.VMEM((far * WIDE + 8, LANES), F32)],
         name="near_sum",
-    )(got)
+    )(near_by(got))
     got = lax.all_to_all(sent, FAR, 0, 0, tiled=True)
     mine = pl.pallas_call(
         far_kernel,
-        out_shape=jax.ShapeDtypeStruct((SECOND, LANES), F32),
+        out_shape=pltpu.VMEM((SECOND, LANES), F32),
         in_specs=vmem(1),
         out_specs=vmem(1)[0],
         name="far_sum",
-    )(got)
+    )(near_by(got))
     theirs = lax.ppermute(mine, "rep", SWAP)
     whitened = pl.pallas_call(
         white_kernel,
@@ -327,18 +335,18 @@
         out_specs=vmem(1)[0],
         cost_estimate=pl.CostEstimate(flops=10**7, transcendentals=0, bytes_accessed=10**6),
         name="white",
-    )(got)
+    )(near_by(got))
     gram, projection = pl.pallas_call(
         join_kernel,
         out_shape=(
-            jax.ShapeDtypeStruct((cols, 2 * cols), F32),
+            jax.ShapeDtypeStruct((cols, 1, 2 * cols), F32),
             jax.ShapeDtypeStruct((1, cols), F32),
         ),
         in_specs=vmem(2),
         out_specs=tuple(vmem(2)),
         name="join",
-    )(mine, theirs)
-    return gram.T[None], projection, whitened
+    )(near_by(mine), near_by(theirs))
+    return jnp.transpose(gram, (1, 2, 0)), projection, whitened
 
 
 def solution(mesh):

time: 72.2 us -> 57.2 us (0.79)
  local copies, waits for them, and re-layouts: 9.85 us -> 0.01 us
  Pallas kernels: 18.4 us -> 14.1 us
    unnamed x21 -> x2, local copies, waits for them, and re-layouts: 9.85 us -> 0.01 us
    pallas_call x3, Pallas kernels: 5.19 us -> 1.13 us  [the longest x1 0.9 us: shards(): pl.pallas_call(join_kernel, out_shape=(jax.ShapeDtypeStruct((cols, 1, 2 *...]
    pallas_call x1, Pallas kernels: 1.83 us -> 0.93 us  [shards(): pl.pallas_call(white_kernel, out_shape=jax.ShapeDtypeStruct((tiles, rows)...]
  transfers between devices with their start and end apart: 2 -> 2, of which waited for: 0 -> 0; matrix products, arithmetic and copies ran while one was open for 0% -> 0% of each run, Pallas kernels for 10% -> 12%
where the time goes in v3:
time: 57.2 us; the launch traced here: 57 us
  blocking collectives  36 us (63%)
  Pallas kernels  14.1 us (25%)
  starting transfers between devices  6.27 us (11%)
  between operations  0.67 us (1%)
    all_to_all x1, blocking collectives, shards(): got = lax.all_to_all(sent, NEAR, 0, 0, tiled=True)  20.1 us
    all_to_all x1, blocking collectives, shards(): got = lax.all_to_all(sent, FAR, 0, 0, tiled=True)  15.9 us
    pallas_call x1, Pallas kernels, shards(): pl.pallas_call(functools.partial(cross_kernel, near, far), out_shape=jax....  6.05 us
    pallas_call x1, Pallas kernels, shards(): pl.pallas_call(functools.partial(own_kernel, near, far), out_shape=(jax.S...  5.99 us
    ppermute x1, starting transfers between devices, shards(): other = lax.ppermute(own, 'rep', SWAP)  3.29 us
    ppermute x1, starting transfers between devices, shards(): theirs = lax.ppermute(mine, 'rep', SWAP)  2.98 us
  transfers between devices with their start and end apart: 2, of which 0 were waited for; matrix products, arithmetic and copies ran while one was open for 0% of the time, Pallas kernels for 12%

profile of v3, /device:TPU:1, one launch (start us, length us, event | category | flops | bytes accessed | tf_op | source)
XLA Modules:
  0.0 57.0 jit_solution(13260422901684968089)
XLA Ops:
  0.6 3.3 %collective-permute-start = (bf16[50,128,256]{2,1,0:T(8,128)(2,1)}, bf16[50,128,256]{2,1,0:T(8,128)(2,1)S(1)}, u32[]{:S(2)}, u32[]{:S(2)}) collective-permute-start(bf16[50,128,256]{2,1,0:T(8,128)(2,1)} %bitcast.10), channel_id=1, source_target_pairs={{0,1},{1,0},{2,3},{3,2},{4,5},{5,4},{6,7},{7,6},{8,9},{9,8},{10,11... | collective-permute-start | bytes 9830408 | tf_op jit(solution)/shard_map/ppermute | solution.py:278
  3.9 0.0 copy-start
  3.9 6.0 %own.1 = (bf16[128,64,256]{2,1,0:T(8,128)(2,1)S(1)}, f32[3584,128]{1,0:T(8,128)S(1)}) custom-call(s32[1,128]{1,0:T(1,128)} %bitcast.8, s32[1,128]{1,0:T(1,128)} %bitcast.15, s32[1,128]{1,0:T(1,128)} %bitcast.16, s32[1,128]{1,0:T(1,128)} %bitcast.17, f32[128,256]{1,0:T(8,128)} %residual_in.1, f32[128,256]{1,0:T(8,128)} %error_in.1, f32[64,128]{1,0:T(8,128)} %bitcast.12, ...), custom_call_target="tpu_custom_call" | custom-call | flops 2000000000 | bytes 10000000 | tf_op jit(solution)/shard_map/own/pallas_call | solution.py:282
  9.9 0.0 collective-permute-done.other
  9.9 0.0 copy-done
  9.9 6.0 %cross.1 = bf16[16,224,128]{2,1,0:T(8,128)(2,1)S(1)} custom-call(s32[1,128]{1,0:T(1,128)S(1)} %bitcast.9, bf16[128,64,256]{2,1,0:T(8,128)(2,1)S(1)} %get-tuple-element.7.left, f32[3584,128]{1,0:T(8,128)S(1)} %get-tuple-element.8.acc_own, bf16[50,128,256]{2,1,0:T(8,128)(2,1)S(1)} %collective-permute-done.other), custom_call_target="tpu_custom_call" | custom-call | tf_op jit(solution)/shard_map/cross/pallas_call | solution.py:304
  16.0 20.1 %all_to_all.10.got = bf16[16,224,128]{2,1,0:T(8,128)(2,1)S(1)} all-to-all(bf16[16,224,128]{2,1,0:T(8,128)(2,1)S(1)} %cross.1), channel_id=1, replica_groups=mesh['toa_0'=8,'toa_1'=4,'toa_2'=4,'rep'=2] {'toa_1','toa_2'}, dimensions={0} | all-to-all | bytes 1835008 | tf_op jit(solution)/shard_map/all_to_all | solution.py:313
  36.1 0.2 near_sum.1
  36.3 15.9 %all_to_all.11.got = bf16[8,64,128]{2,1,0:T(8,128)(2,1)S(1)} all-to-all(bf16[8,64,128]{2,1,0:T(8,128)(2,1)S(1)} %near_sum.1), channel_id=1, replica_groups=mesh['toa_0'=8,'toa_1'=4,'toa_2'=4,'rep'=2] {'toa_0'}, dimensions={0} | all-to-all | bytes 262144 | tf_op jit(solution)/shard_map/all_to_all | solution.py:322
  52.2 3.0 %collective-permute-start.1 = (f32[32,128]{1,0:T(8,128)S(1)}, f32[32,128]{1,0:T(8,128)S(1)}, u32[]{:S(2)}, u32[]{:S(2)}) collective-permute-start(f32[32,128]{1,0:T(8,128)S(1)} %far_sum.1.mine_in), channel_id=1, source_target_pairs={{0,1},{1,0},{2,3},{3,2},{4,5},{5,4},{6,7},{7,6},{8,9},{9,8},{10,11... | collective-permute-start | bytes 49160 | tf_op jit(solution)/shard_map/ppermute | solution.py:330
  55.2 0.9 %white.1 = f32[128,256]{1,0:T(8,128)} custom-call(bf16[8,64,128]{2,1,0:T(8,128)(2,1)S(1)} %all_to_all.11.got), custom_call_target="tpu_custom_call" | custom-call | flops 10000000 | bytes 1000000 | tf_op jit(solution)/shard_map/white/pallas_call | solution.py:331
  56.1 0.0 collective-permute-done.1.theirs_in
  56.1 0.9 %join.1 = (f32[50,1,100]{2,1,0:T(1,128)}, f32[1,50]{1,0:T(1,128)}) custom-call(f32[32,128]{1,0:T(8,128)S(1)} %far_sum.1.mine_in, f32[32,128]{1,0:T(8,128)S(1)} %collective-permute-done.1.theirs_in), custom_call_target="tpu_custom_call" | custom-call | tf_op jit(solution)/shard_map/join/pallas_call | solution.py:339
  (1 shorter events, 0.0 us)
Async XLA Ops:
  0.6 9.3 %collective-permute-start = (bf16[50,128,256]{2,1,0:T(8,128)(2,1)}, bf16[50,128,256]{2,1,0:T(8,128)(2,1)S(1)}, u32[]{:S(2)}, u32[]{:S(2)}) collective-permute-start(bf16[50,128,256]{2,1,0:T(8,128)(2,1)} %bitcast.10), channel_id=1, source_target_pairs={{0,1},{1,0},{2,3},{3,2},{4,5},{5,4},{6,7},{7,6},{8,9},{9,8},{10,11... | collective-permute-start | bytes 9830408 | tf_op jit(solution)/shard_map/ppermute | solution.py:278
  3.9 6.0 %copy-start = (s32[128]{0:T(128)S(1)}, s32[128]{0:T(128)}, u32[]{:S(2)}) copy-start(s32[128]{0:T(128)} %param.14) | copy-start | bytes 1540
  52.2 3.9 %collective-permute-start.1 = (f32[32,128]{1,0:T(8,128)S(1)}, f32[32,128]{1,0:T(8,128)S(1)}, u32[]{:S(2)}, u32[]{:S(2)}) collective-permute-start(f32[32,128]{1,0:T(8,128)S(1)} %far_sum.1.mine_in), channel_id=1, source_target_pairs={{0,1},{1,0},{2,3},{3,2},{4,5},{5,4},{6,7},{7,6},{8,9},{9,8},{10,11... | collective-permute-start | bytes 49160 | tf_op jit(solution)/shard_map/ppermute | solution.py:330

commit v4 on v3

v4 whole, which is shorter than its diff:
```python
import functools

import jax
import jax.numpy as jnp
from jax import lax
from jax.experimental import pallas as pl
from jax.experimental.pallas import tpu as pltpu
from jax.sharding import Mesh
from jax.sharding import PartitionSpec as P

TOA = ("toa_0", "toa_1", "toa_2")
FAR, NEAR = "toa_0", ("toa_1", "toa_2")
BF16, F32 = jnp.bfloat16, jnp.float32
LANES = 128
GROUP = 16

PART = 25
WIDE = PART + 1
SECOND = 32
OWN = 2 * PART
OWN2 = OWN + SECOND
DIAGONAL = ((0, 7, 75), (7, 13, 108), (13, 25, 114))
PLACE = 126
WHITE = 16


def dot(a, b, dims=((1,), (0,)), **kw):
    return lax.dot_general(a, b, (dims, ((), ())), preferred_element_type=F32, **kw)


def iota(shape, dim):
    return lax.broadcasted_iota(jnp.int32, shape, dim)


def as_column(row, lanes):
    square = jnp.broadcast_to(row, (LANES, row.shape[1])).T
    return jnp.concatenate([square] * (lanes // LANES), axis=1)


def base_row(p, near, message, head):
    return (p % near) * message + head + (p // near) * WIDE


def value_lanes(shape):
    lane = iota(shape, 1)
    return ((lane >= OWN) & (lane < OWN + PART)) | ((lane >= OWN2) & (lane < OWN2 + PART))


def split(value):
    here = value_lanes(value.shape)
    rest = jnp.where(here, value - value.astype(BF16).astype(F32), 0.0)
    return jnp.where(here, value, pltpu.roll(rest, LANES // 2, 1))


def own_kernel(
    near, far, pulsar_in, backend_in, counts_in, slot_in, residual_in, error_in, efac_in, equad_in,
    own_in, left_out, acc,
    pulsar, backend, counts, slot, residual, error, efac_t, equad_t, own, pulsar_sm,
    weight_vm, wres_vm, sems, own_sems,
):
    cols, tiles, rows = own.shape
    message = far + far * WIDE
    pulsars, backends = efac_t.shape[1], efac_t.shape[0]
    pairs = (
        (pulsar_in, pulsar), (backend_in, backend), (counts_in, counts), (slot_in, slot),
        (residual_in, residual), (error_in, error), (efac_in, efac_t), (equad_in, equad_t),
        (pulsar_in, pulsar_sm),
    )
    copies = [pltpu.make_async_copy(a, b, sems.at[i]) for i, (a, b) in enumerate(pairs)]

    def own_copy(g):
        here = pl.ds(pl.multiple_of(g * GROUP, GROUP), GROUP)
        return pltpu.make_async_copy(own_in.at[:, here, :], own.at[:, here, :], own_sems.at[g])

    for copy in copies:
        copy.start()
    for g in range(tiles // GROUP):
        own_copy(g).start()
    acc[...] = jnp.zeros_like(acc)
    for copy in copies:
        copy.wait()

    of_pulsar = (iota((pulsars, tiles), 0) == pulsar[...]).astype(F32)
    of_backend = (iota((backends, tiles), 0) == backend[...]).astype(F32)
    high = dict(precision=lax.Precision.HIGHEST)
    factor = jnp.sum(dot(efac_t[...], of_pulsar, **high) * of_backend, axis=0, keepdims=True)
    floor = jnp.sum(dot(equad_t[...], of_pulsar, **high) * of_backend, axis=0, keepdims=True)
    factor2 = as_column(factor * factor, rows)
    floor2 = as_column(floor * floor, rows)
    count = as_column(counts[...].astype(F32), rows)
    valid = iota((tiles, rows), 1).astype(F32) < count
    weight = jnp.where(valid, 1.0 / (factor2 * error[...] ** 2 + floor2), 0.0)
    weight_vm[...] = weight
    wres_vm[...] = (weight * residual[...]).astype(BF16)
    white = jnp.sqrt(weight) * residual[...]
    white = jnp.where(lax.axis_index("rep") == 0, white[:, :LANES], white[:, LANES:])

    me = lax.axis_index("toa_1") * lax.axis_size("toa_2") + lax.axis_index("toa_2")
    dest = slot[...] // tiles
    place = (slot[...] % tiles).astype(F32)
    order = (dest % near) * far + dest // near
    moved = (iota((tiles, tiles), 0) == order).astype(BF16)
    white_to = dot(moved, white.astype(BF16))
    place_to = dot(moved, as_column(place, LANES).astype(BF16))
    place_to = jnp.where(iota(place_to.shape, 1) == PLACE, place_to, 0.0)
    for n in range(near):
        at = n * message
        acc[at : at + far, :] = white_to[n * far : (n + 1) * far, :]
        acc[pl.ds(at + far + me, far, stride=WIDE), :] = place_to[n * far : (n + 1) * far, :]

    lefts = 2 * SECOND
    wide = 80
    lane, row = iota((SECOND, wide), 1), iota((SECOND, wide), 0)
    own_lane = (lane < PART) | ((lane >= SECOND) & (lane < SECOND + PART))
    second = (~own_lane) | (row == PART)
    kept = own_lane | (row != PART)
    is_wres = iota((lefts, rows), 0) == SECOND + PART

    def turn(g, carry):
        t0 = pl.multiple_of(g * GROUP, GROUP)
        here = pl.ds(t0, GROUP)
        own_copy(g).wait()
        slabs = [
            own[:PART, here, :],
            own[PART : PART + 7, here, :],
            own[PART:, here, :],
            wres_vm[here, :].reshape(1, GROUP, rows),
            own[PART + 7 : PART + 13, here, :],
            own[PART + 13 :, here, :],
            jnp.zeros((4, GROUP, rows), BF16),
        ]
        turned = pltpu.einshape("ktr->tkr", jnp.concatenate(slabs, axis=0))
        group_weight = weight_vm[here, :]
        for u in range(GROUP):
            left = turned[u][:lefts]
            scaled = (left.astype(F32) * group_weight[u : u + 1, :]).astype(BF16)
            scaled = jnp.where(is_wres, left, scaled)
            left_out[t0 + u] = scaled
            out = dot(scaled, turned[u], ((1,), (1,)))
            value = jnp.where(kept, jnp.where(second, out[SECOND:], out[:SECOND]), 0.0)
            base = base_row(pulsar_sm[0, t0 + u], near, message, far)
            acc[pl.ds(base, WIDE), OWN : OWN + wide - 4] += value[:WIDE, : wide - 4]
        return carry

    lax.fori_loop(0, tiles // GROUP, turn, 0)
    for n in range(near):
        here = pl.ds(n * message + far + PART, far, stride=WIDE)
        acc[here, :] = split(acc[here, :])


def cross_kernel(near, far, pulsar_sm, left, acc_in, other, out, acc):
    cols, tiles, rows = other.shape
    message = far + far * WIDE
    core = lax.axis_index("rep")
    second = iota((SECOND, cols), 1) >= PART

    def turn(g, carry):
        t0 = pl.multiple_of(g * GROUP, GROUP)
        here = pl.ds(t0, GROUP)
        slabs = [other[pl.ds(PART * core, PART), here, :], other[pl.ds(PART - PART * core, PART), here, :]]
        turned = pltpu.einshape("ktr->tkr", jnp.concatenate(slabs, axis=0))
        for u in range(GROUP):
            product = dot(left[t0 + u], turned[u], ((1,), (1,)))
            value = jnp.where(second, product[SECOND:], product[:SECOND])
            base = base_row(pulsar_sm[0, t0 + u], near, message, far)
            acc[pl.ds(base, PART), :cols] += value[:PART]
        return carry

    lax.fori_loop(0, tiles // GROUP, turn, 0)

    def pack(n, carry):
        out[n] = acc[pl.ds(pl.multiple_of(n * message, 8), message), :].astype(BF16)
        return carry

    lax.fori_loop(0, near, pack, 0)


def near_kernel(far, got, out, total):
    near = got.shape[0]
    part = got[:, :far, :].astype(F32)
    out[:, :near, :] = jnp.swapaxes(part, 0, 1).astype(BF16)
    summed = got[0, far:, :].astype(F32)
    for n in range(1, near):
        summed = summed + got[n, far:, :].astype(F32)
    total[: far * WIDE, :] = summed
    total[far * WIDE :, :] = jnp.zeros((total.shape[0] - far * WIDE, LANES), F32)
    row = iota((SECOND, LANES), 0)
    for f in range(far):
        block = total[f * WIDE : f * WIDE + SECOND, :]
        whole = split(block + pltpu.roll(block, LANES // 2, 1))
        out[f, WHITE:, :] = jnp.where(row == PART, whole, block).astype(BF16)


def far_kernel(got, out):
    far, near = got.shape[0], WHITE
    tiles = far * near
    total = got[0, WHITE:, :].astype(F32)
    for f in range(1, far):
        total = total + got[f, WHITE:, :].astype(F32)
    out[:SECOND, :] = total
    lane = iota((near, LANES), 1)
    puts = []
    for f in range(far):
        value = got[f, WHITE : WHITE + near, :].astype(F32)
        place = jnp.sum(jnp.where(lane == PLACE, value, 0.0), axis=1, keepdims=True)
        puts.append((lane.astype(F32) == place).astype(F32))
    put = jnp.concatenate(puts, axis=0).astype(BF16)
    out[SECOND:, :] = dot(put, got[:, :near, :].reshape(tiles, LANES), ((0,), (0,)))


def join_kernel(mine_in, theirs_in, gram, proj, white):
    mine, theirs = mine_in[:SECOND, :], theirs_in[:SECOND, :]
    lane = iota((SECOND, LANES), 1)

    def square(a):
        return jnp.concatenate([a, jnp.zeros((LANES - SECOND, LANES), F32)], axis=0).T

    turned = square(pltpu.roll(mine, LANES - OWN2, 1))[:SECOND]
    theirs_t = square(theirs)
    theirs_0 = theirs_t[:SECOND]
    theirs_1 = theirs_t[PART : PART + SECOND]

    def laid(pieces):
        value = jnp.zeros((SECOND, LANES), F32)
        for source, start, width, to in pieces:
            moved = pltpu.roll(source, (to - start) % LANES, 1) if to != start else source
            value = jnp.where((lane >= to) & (lane < to + width), moved, value)
        return value

    def write(own, low, high):
        top = [(mine, OWN, PART, own), (mine, OWN2, PART, own + PART)]
        under = [(turned, 0, PART, own)]
        under += [(mine, at, b - a, own + PART + a) for a, b, at in DIAGONAL]
        if own == 0:
            top += [(mine, 0, PART, low), (theirs_1, 0, PART, high)]
            under += [(theirs_0, 0, PART, low), (mine, PART, PART, high)]
        else:
            top += [(theirs_0, 0, PART, low), (mine, 0, PART, high)]
            under += [(mine, PART, PART, low), (theirs_1, 0, PART, high)]
        gram[:PART, 0, :] = laid(top)[:PART, : 4 * PART]
        gram[PART:, 0, :] = laid(under)[:PART, : 4 * PART]
        halves = (mine_in, theirs_in) if own == 0 else (theirs_in, mine_in)
        for i, half in enumerate(halves):
            white[:, i * LANES : (i + 1) * LANES] = half[SECOND:, :]

    core = lax.axis_index("rep")

    @pl.when(core == 0)
    def _():
        write(0, 2 * PART, 3 * PART)

    @pl.when(core == 1)
    def _():
        write(2 * PART, 0, PART)

    sums = mine + pltpu.roll(mine, LANES // 2, 1)
    proj[...] = laid([(sums, OWN, PART, 0), (sums, OWN2, PART, PART)])[PART:WIDE, : 2 * PART]


def vmem(n):
    return [pl.BlockSpec(memory_space=pltpu.VMEM)] * n


SMEM = pl.BlockSpec(memory_space=pltpu.SMEM)
HBM = pl.BlockSpec(memory_space=pltpu.HBM)
SWAP = [(0, 1), (1, 0)]


def stay(a):
    return pltpu.with_memory_space_constraint(a, pltpu.HBM)


def near_by(a):
    return pltpu.with_memory_space_constraint(a, pltpu.VMEM)


def shards(
    residual, toa_error, basis_rows, efac_table, equad_table, pulsar, backend, counts, owner_slot
):
    far, near = lax.axis_size(FAR), lax.axis_size(NEAR)
    tiles, cols, rows = basis_rows.shape
    own = jnp.transpose(basis_rows, (1, 0, 2))
    other = lax.ppermute(own, "rep", SWAP)
    message = far + far * WIDE
    line = lambda a: a.reshape(1, -1)
    ints = [line(a) for a in (pulsar, backend, counts, owner_slot)]
    left, acc = pl.pallas_call(
        functools.partial(own_kernel, near, far),
        out_shape=(
            jax.ShapeDtypeStruct((tiles, 2 * SECOND, rows), BF16),
            jax.ShapeDtypeStruct((near * message, LANES), F32),
        ),
        in_specs=[HBM] * 9,
        out_specs=tuple(vmem(2)),
        scratch_shapes=[pltpu.VMEM((1, tiles), jnp.int32)] * 4
        + [pltpu.VMEM((tiles, rows), F32)] * 2
        + [pltpu.VMEM(efac_table.shape[::-1], F32)] * 2
        + [
            pltpu.VMEM(own.shape, BF16),
            pltpu.SMEM((1, tiles), jnp.int32),
            pltpu.VMEM((tiles, rows), F32),
            pltpu.VMEM((tiles, rows), BF16),
            pltpu.SemaphoreType.DMA((9,)),
            pltpu.SemaphoreType.DMA((tiles // GROUP,)),
        ],
        compiler_params=pltpu.CompilerParams(vmem_limit_bytes=32 << 20),
        cost_estimate=pl.CostEstimate(flops=2 * 10**9, transcendentals=0, bytes_accessed=10**7),
        name="own",
    )(*map(stay, (*ints, residual, toa_error, efac_table.T, equad_table.T, own)))
    sent, _ = pl.pallas_call(
        functools.partial(cross_kernel, near, far),
        out_shape=(
            pltpu.VMEM((near, message, LANES), BF16),
            pltpu.VMEM((near * message, LANES), F32),
        ),
        in_specs=[SMEM] + vmem(3),
        out_specs=tuple(vmem(2)),
        input_output_aliases={2: 1},
        compiler_params=pltpu.CompilerParams(vmem_limit_bytes=32 << 20),
        name="cross",
    )(ints[0], left, acc, other)
    got = lax.all_to_all(sent, NEAR, 0, 0, tiled=True)
    sent = pl.pallas_call(
        functools.partial(near_kernel, far),
        out_shape=pltpu.VMEM((far, WHITE + SECOND, LANES), BF16),
        in_specs=vmem(1),
        out_specs=vmem(1)[0],
        scratch_shapes=[pltpu.VMEM((far * WIDE + 8, LANES), F32)],
        name="near_sum",
    )(near_by(got))
    got = lax.all_to_all(sent, FAR, 0, 0, tiled=True)
    mine = pl.pallas_call(
        far_kernel,
        out_shape=pltpu.VMEM((SECOND + tiles, LANES), F32),
        in_specs=vmem(1),
        out_specs=vmem(1)[0],
        name="far_sum",
    )(near_by(got))
    theirs = lax.ppermute(mine, "rep", SWAP)
    gram, projection, whitened = pl.pallas_call(
        join_kernel,
        out_shape=(
            jax.ShapeDtypeStruct((cols, 1, 2 * cols), F32),
            jax.ShapeDtypeStruct((1, cols), F32),
            jax.ShapeDtypeStruct((tiles, rows), F32),
        ),
        in_specs=vmem(2),
        out_specs=tuple(vmem(3)),
        name="join",
    )(near_by(mine), near_by(theirs))
    return jnp.transpose(gram, (1, 2, 0)), projection, whitened


def solution(mesh):
    split = Mesh(
        mesh.devices.reshape(8, 4, 4, mesh.shape["rep"]), ("toa_0", "toa_1", "toa_2", "rep")
    )
    placed = (
        P(TOA, None),
        P(TOA, None),
        P(TOA, "rep", None),
        P(),
        P(),
        P(TOA),
        P(TOA),
        P(TOA),
        P(TOA),
    )
    return jax.shard_map(
        shards,
        mesh=split,
        in_specs=placed,
        out_specs=(P(TOA, None, "rep"), P(TOA, "rep"), P(TOA, None)),
        check_vma=False,
    )
```

time: 57.2 us -> 54.2 us (0.948)
  Pallas kernels: 14.1 us -> 10.9 us
  waiting for transfers between devices: 0.01 us -> 0.93 us
  blocking collectives: 36 us -> 35.3 us
    pallas_call x3 -> x2, Pallas kernels: 6.99 us -> 3.58 us  [the longest x1 3.32 us: shards(): pl.pallas_call(functools.partial(cross_kernel, near, far), out_shape=(plt...]
    ppermute x1, waiting for transfers between devices: 0.01 us -> 0.92 us  [shards(): theirs = lax.ppermute(mine, 'rep', SWAP)]
  transfers between devices with their start and end apart: 2 -> 2, of which waited for: 0 -> 1; matrix products, arithmetic and copies ran while one was open for 0% -> 0% of each run, Pallas kernels for 12% -> 11%
where the time goes in v4:
time: 54.2 us; the launch traced here: 54.1 us
  blocking collectives  35.3 us (65%)
  Pallas kernels  10.9 us (20%)
  starting transfers between devices  6.25 us (12%)
  waiting for transfers between devices  0.93 us (2%)
  between operations  0.67 us (1%)
    all_to_all x1, blocking collectives, shards(): got = lax.all_to_all(sent, NEAR, 0, 0, tiled=True)  19.7 us
    all_to_all x1, blocking collectives, shards(): got = lax.all_to_all(sent, FAR, 0, 0, tiled=True)  15.5 us
    pallas_call x1, Pallas kernels, shards(): pl.pallas_call(functools.partial(own_kernel, near, far), out_shape=(jax.S...  6.01 us
    pallas_call x1, Pallas kernels, shards(): pl.pallas_call(functools.partial(cross_kernel, near, far), out_shape=(plt...  3.32 us
    ppermute x1, starting transfers between devices, shards(): other = lax.ppermute(own, 'rep', SWAP)  3.29 us
    ppermute x1, starting transfers between devices, shards(): theirs = lax.ppermute(mine, 'rep', SWAP)  2.97 us
  transfers between devices with their start and end apart: 2, of which 1 were waited for; matrix products, arithmetic and copies ran while one was open for 0% of the time, Pallas kernels for 11%

profile of v4, /device:TPU:1, one launch (start us, length us, event | category | flops | bytes accessed | tf_op | source)
XLA Modules:
  0.0 54.1 jit_solution(18297602876692019688)
XLA Ops:
  0.6 3.3 %collective-permute-start = (bf16[50,128,256]{2,1,0:T(8,128)(2,1)}, bf16[50,128,256]{2,1,0:T(8,128)(2,1)S(1)}, u32[]{:S(2)}, u32[]{:S(2)}) collective-permute-start(bf16[50,128,256]{2,1,0:T(8,128)(2,1)} %bitcast.10), channel_id=1, source_target_pairs={{0,1},{1,0},{2,3},{3,2},{4,5},{5,4},{6,7},{7,6},{8,9},{9,8},{10,11... | collective-permute-start | bytes 9830408 | tf_op jit(solution)/shard_map/ppermute | solution.py:283
  3.9 0.0 copy-start
  3.9 6.0 %own.1 = (bf16[128,64,256]{2,1,0:T(8,128)(2,1)S(1)}, f32[3456,128]{1,0:T(8,128)S(1)}) custom-call(s32[1,128]{1,0:T(1,128)} %bitcast.8, s32[1,128]{1,0:T(1,128)} %bitcast.15, s32[1,128]{1,0:T(1,128)} %bitcast.16, s32[1,128]{1,0:T(1,128)} %bitcast.17, f32[128,256]{1,0:T(8,128)} %residual_in.1, f32[128,256]{1,0:T(8,128)} %error_in.1, f32[64,128]{1,0:T(8,128)} %bitcast.12, ...), custom_call_target="tpu_custom_call" | custom-call | flops 2000000000 | bytes 10000000 | tf_op jit(solution)/shard_map/own/pallas_call | solution.py:287
  9.9 0.0 collective-permute-done.other
  10.0 0.0 copy-done
  10.0 3.3 %cross.1 = (bf16[16,216,128]{2,1,0:T(8,128)(2,1)S(1)}, f32[3456,128]{1,0:T(8,128)S(1)}) custom-call(s32[1,128]{1,0:T(1,128)S(1)} %bitcast.9, bf16[128,64,256]{2,1,0:T(8,128)(2,1)S(1)} %get-tuple-element.9.left, f32[3456,128]{1,0:T(8,128)S(1)} %get-tuple-element.10.acc_in, ...), custom_call_target="tpu_custom_call", output_to_operand_aliasing={{1}: (2, {})} | custom-call | tf_op jit(solution)/shard_map/cross/pallas_call | solution.py:310
  13.3 19.7 %all_to_all.10.got = bf16[16,216,128]{2,1,0:T(8,128)(2,1)S(1)} all-to-all(bf16[16,216,128]{2,1,0:T(8,128)(2,1)S(1)} %get-tuple-element.11), channel_id=1, replica_groups=mesh['toa_0'=8,'toa_1'=4,'toa_2'=4,'rep'=2] {'toa_1','toa_2'}, dimensions={0} | all-to-all | bytes 1769472 | tf_op jit(solution)/shard_map/all_to_all | solution.py:322
  33.0 0.3 near_sum.1
  33.3 15.5 %all_to_all.11.got = bf16[8,48,128]{2,1,0:T(8,128)(2,1)S(1)} all-to-all(bf16[8,48,128]{2,1,0:T(8,128)(2,1)S(1)} %near_sum.1), channel_id=1, replica_groups=mesh['toa_0'=8,'toa_1'=4,'toa_2'=4,'rep'=2] {'toa_0'}, dimensions={0} | all-to-all | bytes 196608 | tf_op jit(solution)/shard_map/all_to_all | solution.py:331
  48.9 0.3 far_sum.1.mine_in
  49.1 3.0 %collective-permute-start.1 = (f32[160,128]{1,0:T(8,128)S(1)}, f32[160,128]{1,0:T(8,128)S(1)}, u32[]{:S(2)}, u32[]{:S(2)}) collective-permute-start(f32[160,128]{1,0:T(8,128)S(1)} %far_sum.1.mine_in), channel_id=1, source_target_pairs={{0,1},{1,0},{2,3},{3,2},{4,5},{5,4},{6,7},{7,6},{8,9},{9,8},{10,11... | collective-permute-start | bytes 245768 | tf_op jit(solution)/shard_map/ppermute | solution.py:339
  52.1 0.9 %collective-permute-done.1.theirs_in = f32[160,128]{1,0:T(8,128)S(1)} collective-permute-done((f32[160,128]{1,0:T(8,128)S(1)}, f32[160,128]{1,0:T(8,128)S(1)}, u32[]{:S(2)}, u32[]{:S(2)}) %collective-permute-start.1) | collective-permute-done | bytes 81952 | tf_op jit(solution)/shard_map/ppermute | solution.py:339
  53.0 1.0 %join.1 = (f32[50,1,100]{2,1,0:T(1,128)}, f32[1,50]{1,0:T(1,128)}, f32[128,256]{1,0:T(8,128)}) custom-call(f32[160,128]{1,0:T(8,128)S(1)} %far_sum.1.mine_in, f32[160,128]{1,0:T(8,128)S(1)} %collective-permute-done.1.theirs_in), custom_call_target="tpu_custom_call" | custom-call | tf_op jit(solution)/shard_map/join/pallas_call | solution.py:340
Async XLA Ops:
  0.6 9.3 %collective-permute-start = (bf16[50,128,256]{2,1,0:T(8,128)(2,1)}, bf16[50,128,256]{2,1,0:T(8,128)(2,1)S(1)}, u32[]{:S(2)}, u32[]{:S(2)}) collective-permute-start(bf16[50,128,256]{2,1,0:T(8,128)(2,1)} %bitcast.10), channel_id=1, source_target_pairs={{0,1},{1,0},{2,3},{3,2},{4,5},{5,4},{6,7},{7,6},{8,9},{9,8},{10,11... | collective-permute-start | bytes 9830408 | tf_op jit(solution)/shard_map/ppermute | solution.py:283
  3.9 6.0 %copy-start = (s32[128]{0:T(128)S(1)}, s32[128]{0:T(128)}, u32[]{:S(2)}) copy-start(s32[128]{0:T(128)} %param.14) | copy-start | bytes 1540
  49.1 3.9 %collective-permute-start.1 = (f32[160,128]{1,0:T(8,128)S(1)}, f32[160,128]{1,0:T(8,128)S(1)}, u32[]{:S(2)}, u32[]{:S(2)}) collective-permute-start(f32[160,128]{1,0:T(8,128)S(1)} %far_sum.1.mine_in), channel_id=1, source_target_pairs={{0,1},{1,0},{2,3},{3,2},{4,5},{5,4},{6,7},{7,6},{8,9},{9,8},{10,11... | collective-permute-start | bytes 245768 | tf_op jit(solution)/shard_map/ppermute | solution.py:339

commit v5 on v4

--- a/solution.py
+++ b/solution.py
@@ -19,8 +19,10 @@
 SECOND = 32
 OWN = 2 * PART
 OWN2 = OWN + SECOND
-DIAGONAL = ((0, 7, 75), (7, 13, 108), (13, 25, 114))
+USED = OWN2 + WIDE
+PIECE = 18
 PLACE = 126
+LAST_PLACE = 124
 WHITE = 16
 
 
@@ -41,15 +43,24 @@
     return (p % near) * message + head + (p // near) * WIDE
 
 
-def value_lanes(shape):
-    lane = iota(shape, 1)
-    return ((lane >= OWN) & (lane < OWN + PART)) | ((lane >= OWN2) & (lane < OWN2 + PART))
-
-
 def split(value):
-    here = value_lanes(value.shape)
-    rest = jnp.where(here, value - value.astype(BF16).astype(F32), 0.0)
-    return jnp.where(here, value, pltpu.roll(rest, LANES // 2, 1))
+    lane = iota(value.shape, 1)
+    rest = value - value.astype(BF16).astype(F32)
+    first = pltpu.roll(rest, LANES - OWN - 1, 1)
+    second = pltpu.roll(rest, LANES - (OWN2 + 1 - PART), 1)
+    return jnp.where(lane < PART, first, jnp.where(lane < OWN, second, value))
+
+
+def joined(value):
+    lane = iota(value.shape, 1)
+    first = pltpu.roll(value, OWN + 1, 1)
+    second = pltpu.roll(value, OWN2 + 1 - PART, 1)
+    return value + jnp.where(lane < OWN2, first, second)
+
+
+def message_rows(far):
+    rows = far + (far - 1) * WIDE
+    return rows + -rows % 8
 
 
 def own_kernel(
@@ -59,7 +70,7 @@
     weight_vm, wres_vm, sems, own_sems,
 ):
     cols, tiles, rows = own.shape
-    message = far + far * WIDE
+    block = far + far * WIDE
     pulsars, backends = efac_t.shape[1], efac_t.shape[0]
     pairs = (
         (pulsar_in, pulsar), (backend_in, backend), (counts_in, counts), (slot_in, slot),
@@ -104,55 +115,61 @@
     place_to = dot(moved, as_column(place, LANES).astype(BF16))
     place_to = jnp.where(iota(place_to.shape, 1) == PLACE, place_to, 0.0)
     for n in range(near):
-        at = n * message
+        at = n * block
         acc[at : at + far, :] = white_to[n * far : (n + 1) * far, :]
         acc[pl.ds(at + far + me, far, stride=WIDE), :] = place_to[n * far : (n + 1) * far, :]
 
     lefts = 2 * SECOND
-    wide = 80
-    lane, row = iota((SECOND, wide), 1), iota((SECOND, wide), 0)
-    own_lane = (lane < PART) | ((lane >= SECOND) & (lane < SECOND + PART))
-    second = (~own_lane) | (row == PART)
-    kept = own_lane | (row != PART)
-    is_wres = iota((lefts, rows), 0) == SECOND + PART
+    lane, row = iota((SECOND, lefts), 1), iota((SECOND, lefts), 0)
+    lower = (row > 0) & (lane < row) & (lane < PART)
+    projected = (row == 0) & (((lane > 0) & (lane < WIDE)) | (lane > SECOND))
+    kept = ((row > 0) & (lane != SECOND)) | projected
+    is_wres = iota((GROUP, rows), 0) == 0
 
     def turn(g, carry):
         t0 = pl.multiple_of(g * GROUP, GROUP)
         here = pl.ds(t0, GROUP)
         own_copy(g).wait()
+        none = lambda n: jnp.zeros((n, GROUP, rows), BF16)
         slabs = [
+            none(1),
             own[:PART, here, :],
-            own[PART : PART + 7, here, :],
+            none(SECOND - WIDE),
+            wres_vm[here, :].reshape(1, GROUP, rows),
             own[PART:, here, :],
-            wres_vm[here, :].reshape(1, GROUP, rows),
-            own[PART + 7 : PART + 13, here, :],
-            own[PART + 13 :, here, :],
-            jnp.zeros((4, GROUP, rows), BF16),
+            none(SECOND - WIDE),
         ]
         turned = pltpu.einshape("ktr->tkr", jnp.concatenate(slabs, axis=0))
         group_weight = weight_vm[here, :]
         for u in range(GROUP):
-            left = turned[u][:lefts]
-            scaled = (left.astype(F32) * group_weight[u : u + 1, :]).astype(BF16)
-            scaled = jnp.where(is_wres, left, scaled)
-            left_out[t0 + u] = scaled
-            out = dot(scaled, turned[u], ((1,), (1,)))
-            value = jnp.where(kept, jnp.where(second, out[SECOND:], out[:SECOND]), 0.0)
-            base = base_row(pulsar_sm[0, t0 + u], near, message, far)
-            acc[pl.ds(base, WIDE), OWN : OWN + wide - 4] += value[:WIDE, : wide - 4]
+            right = turned[u]
+            left = (right.astype(F32) * group_weight[u : u + 1, :]).astype(BF16)
+            middle = slice(SECOND, SECOND + GROUP)
+            middle = jnp.where(is_wres, right[middle], left[middle])
+            left = jnp.concatenate([left[:SECOND], middle, left[SECOND + GROUP :]], axis=0)
+            left_out[t0 + u] = left
+            out = dot(left, right, ((1,), (1,)))
+            low, high = out[:SECOND], out[SECOND:]
+            moved = jnp.concatenate([high[:, SECOND + 1 :], high[:, : SECOND + 1]], axis=1)
+            value = jnp.where(lower, moved, jnp.where(projected, high, low))
+            value = jnp.where(kept, value, 0.0)
+            base = base_row(pulsar_sm[0, t0 + u], near, block, far)
+            acc[pl.ds(base, WIDE), OWN:USED] += value[:WIDE, : USED - OWN]
         return carry
 
     lax.fori_loop(0, tiles // GROUP, turn, 0)
     for n in range(near):
-        here = pl.ds(n * message + far + PART, far, stride=WIDE)
+        here = pl.ds(n * block + far, far, stride=WIDE)
         acc[here, :] = split(acc[here, :])
 
 
 def cross_kernel(near, far, pulsar_sm, left, acc_in, other, out, acc):
     cols, tiles, rows = other.shape
-    message = far + far * WIDE
+    block = far + far * WIDE
+    message = out.shape[1]
     core = lax.axis_index("rep")
-    second = iota((SECOND, cols), 1) >= PART
+    lane, row = iota((SECOND, cols), 1), iota((SECOND, cols), 0)
+    second = (lane >= PART) & (row > 0)
 
     def turn(g, carry):
         t0 = pl.multiple_of(g * GROUP, GROUP)
@@ -162,17 +179,29 @@
         for u in range(GROUP):
             product = dot(left[t0 + u], turned[u], ((1,), (1,)))
             value = jnp.where(second, product[SECOND:], product[:SECOND])
-            base = base_row(pulsar_sm[0, t0 + u], near, message, far)
-            acc[pl.ds(base, PART), :cols] += value[:PART]
+            base = base_row(pulsar_sm[0, t0 + u], near, block, far)
+            acc[pl.ds(base, WIDE), :cols] += value[:WIDE]
         return carry
 
     lax.fori_loop(0, tiles // GROUP, turn, 0)
 
+    lane = iota((WIDE, LANES), 1)
+
     def pack(n, carry):
-        out[n] = acc[pl.ds(pl.multiple_of(n * message, 8), message), :].astype(BF16)
+        at = pl.multiple_of(n * block, 8)
+        last = acc[pl.ds(at + far + (far - 1) * WIDE, WIDE), :]
+        for i in range(far - 1):
+            here = pl.ds(at + far + i * WIDE, WIDE)
+            if i < USED // PIECE:
+                moved = pltpu.roll(last, USED - i * PIECE, 1)
+                acc[here, USED : USED + PIECE] = moved[:, USED : USED + PIECE]
+            else:
+                moved = pltpu.roll(last, LANES - (PLACE - LAST_PLACE), 1)
+                acc[here, LAST_PLACE : LAST_PLACE + 1] = moved[:, LAST_PLACE : LAST_PLACE + 1]
+        out[n] = acc[pl.ds(at, message), :].astype(BF16)
         return carry
 
-    lax.fori_loop(0, near, pack, 0)
+    lax.fori_loop(0, near, pack, 0, unroll=4)
 
 
 def near_kernel(far, got, out, total):
@@ -182,13 +211,23 @@
     summed = got[0, far:, :].astype(F32)
     for n in range(1, near):
         summed = summed + got[n, far:, :].astype(F32)
-    total[: far * WIDE, :] = summed
-    total[far * WIDE :, :] = jnp.zeros((total.shape[0] - far * WIDE, LANES), F32)
-    row = iota((SECOND, LANES), 0)
+    total[: summed.shape[0], :] = summed
+    total[summed.shape[0] :, :] = jnp.zeros((total.shape[0] - summed.shape[0], LANES), F32)
+    lane, row = iota((SECOND, LANES), 1), iota((SECOND, LANES), 0)
+    last = jnp.zeros((SECOND, LANES), F32)
     for f in range(far):
-        block = total[f * WIDE : f * WIDE + SECOND, :]
-        whole = split(block + pltpu.roll(block, LANES // 2, 1))
-        out[f, WHITE:, :] = jnp.where(row == PART, whole, block).astype(BF16)
+        if f < far - 1:
+            block = total[f * WIDE : f * WIDE + SECOND, :]
+            if f < USED // PIECE:
+                moved = pltpu.roll(block, LANES - (USED - f * PIECE), 1)
+                last = jnp.where((lane >= f * PIECE) & (lane < (f + 1) * PIECE), moved, last)
+            else:
+                last = jnp.where(lane == PLACE, pltpu.roll(block, PLACE - LAST_PLACE, 1), last)
+        else:
+            block = last
+        whole = split(joined(block))
+        whole = jnp.where(lane == PLACE, block, whole)
+        out[f, WHITE:, :] = jnp.where(row == 0, whole, block).astype(BF16)
 
 
 def far_kernel(got, out):
@@ -208,35 +247,39 @@
     out[SECOND:, :] = dot(put, got[:, :near, :].reshape(tiles, LANES), ((0,), (0,)))
 
 
-def join_kernel(mine_in, theirs_in, gram, proj, white):
-    mine, theirs = mine_in[:SECOND, :], theirs_in[:SECOND, :]
-    lane = iota((SECOND, LANES), 1)
+def join_kernel(mine_in, theirs_in, gram, proj, white, mine_t, theirs_t):
+    lane, row = iota((SECOND, LANES), 1), iota((SECOND, LANES), 0)
+    mine = mine_in[1 : SECOND + 1, :]
 
     def square(a):
         return jnp.concatenate([a, jnp.zeros((LANES - SECOND, LANES), F32)], axis=0).T
 
-    turned = square(pltpu.roll(mine, LANES - OWN2, 1))[:SECOND]
-    theirs_t = square(theirs)
-    theirs_0 = theirs_t[:SECOND]
-    theirs_1 = theirs_t[PART : PART + SECOND]
+    mine_t[...] = square(mine)
+    theirs_t[...] = square(theirs_in[1 : SECOND + 1, :])
+    low = pltpu.roll(mine, LANES - OWN - 1, 1)
+    first = jnp.where(lane >= row, low, mine_t[OWN + 1 : OWN + SECOND + 1, :])
+    high = pltpu.roll(mine, LANES - OWN, 1)
+    second = jnp.where(lane <= row, high, mine_t[OWN : OWN + SECOND, :])
+    turned = mine_t[OWN2 + 1 : OWN2 + SECOND + 1, :]
+    theirs_0 = theirs_t[:SECOND, :]
+    theirs_1 = theirs_t[PART : PART + SECOND, :]
 
     def laid(pieces):
         value = jnp.zeros((SECOND, LANES), F32)
-        for source, start, width, to in pieces:
+        for source, start, to in pieces:
             moved = pltpu.roll(source, (to - start) % LANES, 1) if to != start else source
-            value = jnp.where((lane >= to) & (lane < to + width), moved, value)
+            value = jnp.where((lane >= to) & (lane < to + PART), moved, value)
         return value
 
     def write(own, low, high):
-        top = [(mine, OWN, PART, own), (mine, OWN2, PART, own + PART)]
-        under = [(turned, 0, PART, own)]
-        under += [(mine, at, b - a, own + PART + a) for a, b, at in DIAGONAL]
+        top = [(first, 0, own), (mine, OWN2 + 1, own + PART)]
+        under = [(turned, 0, own), (second, 0, own + PART)]
         if own == 0:
-            top += [(mine, 0, PART, low), (theirs_1, 0, PART, high)]
-            under += [(theirs_0, 0, PART, low), (mine, PART, PART, high)]
+            top += [(mine, 0, low), (theirs_1, 0, high)]
+            under += [(theirs_0, 0, low), (mine, PART, high)]
         else:
-            top += [(theirs_0, 0, PART, low), (mine, 0, PART, high)]
-            under += [(mine, PART, PART, low), (theirs_1, 0, PART, high)]
+            top += [(theirs_0, 0, low), (mine, 0, high)]
+            under += [(mine, PART, low), (theirs_1, 0, high)]
         gram[:PART, 0, :] = laid(top)[:PART, : 4 * PART]
         gram[PART:, 0, :] = laid(under)[:PART, : 4 * PART]
         halves = (mine_in, theirs_in) if own == 0 else (theirs_in, mine_in)
@@ -253,8 +296,8 @@
     def _():
         write(2 * PART, 0, PART)
 
-    sums = mine + pltpu.roll(mine, LANES // 2, 1)
-    proj[...] = laid([(sums, OWN, PART, 0), (sums, OWN2, PART, PART)])[PART:WIDE, : 2 * PART]
+    sums = joined(mine_in[:SECOND, :])
+    proj[...] = laid([(sums, OWN + 1, 0), (sums, OWN2 + 1, PART)])[:1, : 2 * PART]
 
 
 def vmem(n):
@@ -281,14 +324,15 @@
     tiles, cols, rows = basis_rows.shape
     own = jnp.transpose(basis_rows, (1, 0, 2))
     other = lax.ppermute(own, "rep", SWAP)
-    message = far + far * WIDE
+    block = far + far * WIDE
+    message = message_rows(far)
     line = lambda a: a.reshape(1, -1)
     ints = [line(a) for a in (pulsar, backend, counts, owner_slot)]
     left, acc = pl.pallas_call(
         functools.partial(own_kernel, near, far),
         out_shape=(
             jax.ShapeDtypeStruct((tiles, 2 * SECOND, rows), BF16),
-            jax.ShapeDtypeStruct((near * message, LANES), F32),
+            jax.ShapeDtypeStruct((near * block, LANES), F32),
         ),
         in_specs=[HBM] * 9,
         out_specs=tuple(vmem(2)),
@@ -311,7 +355,7 @@
         functools.partial(cross_kernel, near, far),
         out_shape=(
             pltpu.VMEM((near, message, LANES), BF16),
-            pltpu.VMEM((near * message, LANES), F32),
+            pltpu.VMEM((near * block, LANES), F32),
         ),
         in_specs=[SMEM] + vmem(3),
         out_specs=tuple(vmem(2)),
@@ -325,7 +369,7 @@
         out_shape=pltpu.VMEM((far, WHITE + SECOND, LANES), BF16),
         in_specs=vmem(1),
         out_specs=vmem(1)[0],
-        scratch_shapes=[pltpu.VMEM((far * WIDE + 8, LANES), F32)],
+        scratch_shapes=[pltpu.VMEM((message, LANES), F32)],
         name="near_sum",
     )(near_by(got))
     got = lax.all_to_all(sent, FAR, 0, 0, tiled=True)
@@ -346,6 +390,7 @@
         ),
         in_specs=vmem(2),
         out_specs=tuple(vmem(3)),
+        scratch_shapes=[pltpu.VMEM((LANES, LANES), F32)] * 2,
         name="join",
     )(near_by(mine), near_by(theirs))
     return jnp.transpose(gram, (1, 2, 0)), projection, whitened

time: 54.2 us -> 54.3 us (level)
  Pallas kernels: 10.9 us -> 12 us
  blocking collectives: 35.3 us -> 34.5 us
    pallas_call x1, Pallas kernels: 3.32 us -> 4.12 us  [shards(): pl.pallas_call(functools.partial(cross_kernel, near, far), out_shape=(plt...]
    all_to_all x1, blocking collectives: 19.7 us -> 19 us  [shards(): got = lax.all_to_all(sent, NEAR, 0, 0, tiled=True)]
  transfers between devices with their start and end apart: 2 -> 2, of which waited for: 1 -> 1; matrix products, arithmetic and copies ran while one was open for 0% -> 0% of each run, Pallas kernels for 11% -> 12%
where the time goes in v5:
time: 54.3 us; the launch traced here: 54.1 us
  blocking collectives  34.5 us (64%)
  Pallas kernels  12 us (22%)
  starting transfers between devices  5.96 us (11%)
  waiting for transfers between devices  0.93 us (2%)
  between operations  0.67 us (1%)
    all_to_all x1, blocking collectives, shards(): got = lax.all_to_all(sent, NEAR, 0, 0, tiled=True)  19 us
    all_to_all x1, blocking collectives, shards(): got = lax.all_to_all(sent, FAR, 0, 0, tiled=True)  15.6 us
    pallas_call x1, Pallas kernels, shards(): pl.pallas_call(functools.partial(own_kernel, near, far), out_shape=(jax.S...  6.29 us
    pallas_call x1, Pallas kernels, shards(): pl.pallas_call(functools.partial(cross_kernel, near, far), out_shape=(plt...  4.12 us
    ppermute x1, starting transfers between devices, shards(): other = lax.ppermute(own, 'rep', SWAP)  3.29 us
    ppermute x1, starting transfers between devices, shards(): theirs = lax.ppermute(mine, 'rep', SWAP)  2.67 us
  transfers between devices with their start and end apart: 2, of which 1 were waited for; matrix products, arithmetic and copies ran while one was open for 0% of the time, Pallas kernels for 12%

profile of v5, /device:TPU:1, one launch (start us, length us, event | category | flops | bytes accessed | tf_op | source)
XLA Modules:
  0.0 54.1 jit_solution(1718685469608191778)
XLA Ops:
  0.6 3.3 %collective-permute-start = (bf16[50,128,256]{2,1,0:T(8,128)(2,1)}, bf16[50,128,256]{2,1,0:T(8,128)(2,1)S(1)}, u32[]{:S(2)}, u32[]{:S(2)}) collective-permute-start(bf16[50,128,256]{2,1,0:T(8,128)(2,1)} %bitcast.10), channel_id=1, source_target_pairs={{0,1},{1,0},{2,3},{3,2},{4,5},{5,4},{6,7},{7,6},{8,9},{9,8},{10,11... | collective-permute-start | bytes 9830408 | tf_op jit(solution)/shard_map/ppermute | solution.py:326
  3.9 0.0 copy-start
  3.9 6.3 %own.1 = (bf16[128,64,256]{2,1,0:T(8,128)(2,1)S(1)}, f32[3456,128]{1,0:T(8,128)S(1)}) custom-call(s32[1,128]{1,0:T(1,128)} %bitcast.8, s32[1,128]{1,0:T(1,128)} %bitcast.15, s32[1,128]{1,0:T(1,128)} %bitcast.16, s32[1,128]{1,0:T(1,128)} %bitcast.17, f32[128,256]{1,0:T(8,128)} %residual_in.1, f32[128,256]{1,0:T(8,128)} %error_in.1, f32[64,128]{1,0:T(8,128)} %bitcast.12, ...), custom_call_target="tpu_custom_call" | custom-call | flops 2000000000 | bytes 10000000 | tf_op jit(solution)/shard_map/own/pallas_call | solution.py:331
  10.2 0.0 collective-permute-done.other
  10.2 0.0 copy-done
  10.2 4.1 %cross.1 = (bf16[16,192,128]{2,1,0:T(8,128)(2,1)S(1)}, f32[3456,128]{1,0:T(8,128)S(1)}) custom-call(s32[1,128]{1,0:T(1,128)S(1)} %bitcast.9, bf16[128,64,256]{2,1,0:T(8,128)(2,1)S(1)} %get-tuple-element.9.left, f32[3456,128]{1,0:T(8,128)S(1)} %get-tuple-element.10.acc_in, ...), custom_call_target="tpu_custom_call", output_to_operand_aliasing={{1}: (2, {})} | custom-call | tf_op jit(solution)/shard_map/cross/pallas_call | solution.py:354
  14.4 19.0 %all_to_all.10.got = bf16[16,192,128]{2,1,0:T(8,128)(2,1)S(1)} all-to-all(bf16[16,192,128]{2,1,0:T(8,128)(2,1)S(1)} %get-tuple-element.11), channel_id=1, replica_groups=mesh['toa_0'=8,'toa_1'=4,'toa_2'=4,'rep'=2] {'toa_1','toa_2'}, dimensions={0} | all-to-all | bytes 1572864 | tf_op jit(solution)/shard_map/all_to_all | solution.py:366
  33.4 0.3 near_sum.1
  33.7 15.6 %all_to_all.11.got = bf16[8,48,128]{2,1,0:T(8,128)(2,1)S(1)} all-to-all(bf16[8,48,128]{2,1,0:T(8,128)(2,1)S(1)} %near_sum.1), channel_id=1, replica_groups=mesh['toa_0'=8,'toa_1'=4,'toa_2'=4,'rep'=2] {'toa_0'}, dimensions={0} | all-to-all | bytes 196608 | tf_op jit(solution)/shard_map/all_to_all | solution.py:375
  49.2 0.3 far_sum.1.mine_in
  49.5 2.7 %collective-permute-start.1 = (f32[160,128]{1,0:T(8,128)S(1)}, f32[160,128]{1,0:T(8,128)S(1)}, u32[]{:S(2)}, u32[]{:S(2)}) collective-permute-start(f32[160,128]{1,0:T(8,128)S(1)} %far_sum.1.mine_in), channel_id=1, source_target_pairs={{0,1},{1,0},{2,3},{3,2},{4,5},{5,4},{6,7},{7,6},{8,9},{9,8},{10,11... | collective-permute-start | bytes 245768 | tf_op jit(solution)/shard_map/ppermute | solution.py:383
  52.2 0.9 %collective-permute-done.1.theirs_in = f32[160,128]{1,0:T(8,128)S(1)} collective-permute-done((f32[160,128]{1,0:T(8,128)S(1)}, f32[160,128]{1,0:T(8,128)S(1)}, u32[]{:S(2)}, u32[]{:S(2)}) %collective-permute-start.1) | collective-permute-done | bytes 81952 | tf_op jit(solution)/shard_map/ppermute | solution.py:383
  53.1 1.0 %join.1 = (f32[50,1,100]{2,1,0:T(1,128)}, f32[1,50]{1,0:T(1,128)}, f32[128,256]{1,0:T(8,128)}) custom-call(f32[160,128]{1,0:T(8,128)S(1)} %far_sum.1.mine_in, f32[160,128]{1,0:T(8,128)S(1)} %collective-permute-done.1.theirs_in), custom_call_target="tpu_custom_call" | custom-call | tf_op jit(solution)/shard_map/join/pallas_call | solution.py:384
Async XLA Ops:
  0.6 9.6 %collective-permute-start = (bf16[50,128,256]{2,1,0:T(8,128)(2,1)}, bf16[50,128,256]{2,1,0:T(8,128)(2,1)S(1)}, u32[]{:S(2)}, u32[]{:S(2)}) collective-permute-start(bf16[50,128,256]{2,1,0:T(8,128)(2,1)} %bitcast.10), channel_id=1, source_target_pairs={{0,1},{1,0},{2,3},{3,2},{4,5},{5,4},{6,7},{7,6},{8,9},{9,8},{10,11... | collective-permute-start | bytes 9830408 | tf_op jit(solution)/shard_map/ppermute | solution.py:326
  3.9 6.3 %copy-start = (s32[128]{0:T(128)S(1)}, s32[128]{0:T(128)}, u32[]{:S(2)}) copy-start(s32[128]{0:T(128)} %param.14) | copy-start | bytes 1540
  49.5 3.6 %collective-permute-start.1 = (f32[160,128]{1,0:T(8,128)S(1)}, f32[160,128]{1,0:T(8,128)S(1)}, u32[]{:S(2)}, u32[]{:S(2)}) collective-permute-start(f32[160,128]{1,0:T(8,128)S(1)} %far_sum.1.mine_in), channel_id=1, source_target_pairs={{0,1},{1,0},{2,3},{3,2},{4,5},{5,4},{6,7},{7,6},{8,9},{9,8},{10,11... | collective-permute-start | bytes 245768 | tf_op jit(solution)/shard_map/ppermute | solution.py:383

commit v6 on v5

--- a/solution.py
+++ b/solution.py
@@ -40,7 +40,7 @@
 
 
 def base_row(p, near, message, head):
-    return (p % near) * message + head + (p // near) * WIDE
+    return (p & (near - 1)) * message + head + (p >> (near.bit_length() - 1)) * WIDE
 
 
 def split(value):
@@ -73,8 +73,8 @@
     block = far + far * WIDE
     pulsars, backends = efac_t.shape[1], efac_t.shape[0]
     pairs = (
-        (pulsar_in, pulsar), (backend_in, backend), (counts_in, counts), (slot_in, slot),
-        (residual_in, residual), (error_in, error), (efac_in, efac_t), (equad_in, equad_t),
+        (pulsar_in, pulsar), (backend_in, backend), (efac_in, efac_t), (equad_in, equad_t),
+        (counts_in, counts), (error_in, error), (residual_in, residual), (slot_in, slot),
         (pulsar_in, pulsar_sm),
     )
     copies = [pltpu.make_async_copy(a, b, sems.at[i]) for i, (a, b) in enumerate(pairs)]
@@ -88,7 +88,7 @@
     for g in range(tiles // GROUP):
         own_copy(g).start()
     acc[...] = jnp.zeros_like(acc)
-    for copy in copies:
+    for copy in copies[:4]:
         copy.wait()
 
     of_pulsar = (iota((pulsars, tiles), 0) == pulsar[...]).astype(F32)
@@ -98,6 +98,8 @@
     floor = jnp.sum(dot(equad_t[...], of_pulsar, **high) * of_backend, axis=0, keepdims=True)
     factor2 = as_column(factor * factor, rows)
     floor2 = as_column(floor * floor, rows)
+    for copy in copies[4:7]:
+        copy.wait()
     count = as_column(counts[...].astype(F32), rows)
     valid = iota((tiles, rows), 1).astype(F32) < count
     weight = jnp.where(valid, 1.0 / (factor2 * error[...] ** 2 + floor2), 0.0)
@@ -107,6 +109,7 @@
     white = jnp.where(lax.axis_index("rep") == 0, white[:, :LANES], white[:, LANES:])
 
     me = lax.axis_index("toa_1") * lax.axis_size("toa_2") + lax.axis_index("toa_2")
+    copies[7].wait()
     dest = slot[...] // tiles
     place = (slot[...] % tiles).astype(F32)
     order = (dest % near) * far + dest // near
@@ -119,12 +122,14 @@
         acc[at : at + far, :] = white_to[n * far : (n + 1) * far, :]
         acc[pl.ds(at + far + me, far, stride=WIDE), :] = place_to[n * far : (n + 1) * far, :]
 
+    copies[8].wait()
+
     lefts = 2 * SECOND
     lane, row = iota((SECOND, lefts), 1), iota((SECOND, lefts), 0)
     lower = (row > 0) & (lane < row) & (lane < PART)
-    projected = (row == 0) & (((lane > 0) & (lane < WIDE)) | (lane > SECOND))
-    kept = ((row > 0) & (lane != SECOND)) | projected
+    projected = row == 0
     is_wres = iota((GROUP, rows), 0) == 0
+    beyond = jnp.zeros((SECOND, SECOND + 1), F32)
 
     def turn(g, carry):
         t0 = pl.multiple_of(g * GROUP, GROUP)
@@ -150,9 +155,8 @@
             left_out[t0 + u] = left
             out = dot(left, right, ((1,), (1,)))
             low, high = out[:SECOND], out[SECOND:]
-            moved = jnp.concatenate([high[:, SECOND + 1 :], high[:, : SECOND + 1]], axis=1)
+            moved = jnp.concatenate([high[:, SECOND + 1 :], beyond], axis=1)
             value = jnp.where(lower, moved, jnp.where(projected, high, low))
-            value = jnp.where(kept, value, 0.0)
             base = base_row(pulsar_sm[0, t0 + u], near, block, far)
             acc[pl.ds(base, WIDE), OWN:USED] += value[:WIDE, : USED - OWN]
         return carry
@@ -163,13 +167,15 @@
         acc[here, :] = split(acc[here, :])
 
 
-def cross_kernel(near, far, pulsar_sm, left, acc_in, other, out, acc):
+def cross_kernel(near, far, pulsar, left, acc_in, other, out, acc):
     cols, tiles, rows = other.shape
     block = far + far * WIDE
     message = out.shape[1]
     core = lax.axis_index("rep")
     lane, row = iota((SECOND, cols), 1), iota((SECOND, cols), 0)
     second = (lane >= PART) & (row > 0)
+    bases = base_row(pulsar[...], near, block, far).astype(F32)
+    tile = iota(bases.shape, 1)
 
     def turn(g, carry):
         t0 = pl.multiple_of(g * GROUP, GROUP)
@@ -179,29 +185,33 @@
         for u in range(GROUP):
             product = dot(left[t0 + u], turned[u], ((1,), (1,)))
             value = jnp.where(second, product[SECOND:], product[:SECOND])
-            base = base_row(pulsar_sm[0, t0 + u], near, block, far)
+            base = jnp.sum(jnp.where(tile == t0 + u, bases, 0.0)).astype(jnp.int32)
             acc[pl.ds(base, WIDE), :cols] += value[:WIDE]
         return carry
 
     lax.fori_loop(0, tiles // GROUP, turn, 0)
 
     lane = iota((WIDE, LANES), 1)
-
-    def pack(n, carry):
-        at = pl.multiple_of(n * block, 8)
-        last = acc[pl.ds(at + far + (far - 1) * WIDE, WIDE), :]
+    spare = (lane >= USED) & (lane < USED + PIECE)
+
+    def fold(n, carry):
+        at = n * block + far
+        last = acc[pl.ds(at + (far - 1) * WIDE, SECOND), :].astype(BF16)
         for i in range(far - 1):
-            here = pl.ds(at + far + i * WIDE, WIDE)
+            here = acc.at[pl.ds(at + i * WIDE, WIDE), :]
             if i < USED // PIECE:
-                moved = pltpu.roll(last, USED - i * PIECE, 1)
-                acc[here, USED : USED + PIECE] = moved[:, USED : USED + PIECE]
+                pltpu.store(here, pltpu.roll(last, USED - i * PIECE, 1).astype(F32)[:WIDE], mask=spare)
             else:
-                moved = pltpu.roll(last, LANES - (PLACE - LAST_PLACE), 1)
-                acc[here, LAST_PLACE : LAST_PLACE + 1] = moved[:, LAST_PLACE : LAST_PLACE + 1]
-        out[n] = acc[pl.ds(at, message), :].astype(BF16)
+                place = pltpu.roll(last, LANES - (PLACE - LAST_PLACE), 1).astype(F32)[:WIDE]
+                pltpu.store(here, place, mask=lane == LAST_PLACE)
         return carry
 
-    lax.fori_loop(0, near, pack, 0, unroll=4)
+    def convert(n, carry):
+        out[n] = acc[pl.ds(pl.multiple_of(n * block, 8), message), :].astype(BF16)
+        return carry
+
+    lax.fori_loop(0, near, fold, 0, unroll=4)
+    lax.fori_loop(0, near, convert, 0, unroll=2)
 
 
 def near_kernel(far, got, out, total):
@@ -304,7 +314,6 @@
     return [pl.BlockSpec(memory_space=pltpu.VMEM)] * n
 
 
-SMEM = pl.BlockSpec(memory_space=pltpu.SMEM)
 HBM = pl.BlockSpec(memory_space=pltpu.HBM)
 SWAP = [(0, 1), (1, 0)]
 
@@ -332,7 +341,7 @@
         functools.partial(own_kernel, near, far),
         out_shape=(
             jax.ShapeDtypeStruct((tiles, 2 * SECOND, rows), BF16),
-            jax.ShapeDtypeStruct((near * block, LANES), F32),
+            jax.ShapeDtypeStruct((near * block + 8, LANES), F32),
         ),
         in_specs=[HBM] * 9,
         out_specs=tuple(vmem(2)),
@@ -355,9 +364,9 @@
         functools.partial(cross_kernel, near, far),
         out_shape=(
             pltpu.VMEM((near, message, LANES), BF16),
-            pltpu.VMEM((near * block, LANES), F32),
+            pltpu.VMEM((near * block + 8, LANES), F32),
         ),
-        in_specs=[SMEM] + vmem(3),
+        in_specs=vmem(4),
         out_specs=tuple(vmem(2)),
         input_output_aliases={2: 1},
         compiler_params=pltpu.CompilerParams(vmem_limit_bytes=32 << 20),

time: 54.3 us -> 53.3 us (0.982)
  Pallas kernels: 12 us -> 11.1 us
    pallas_call x1, Pallas kernels: 4.12 us -> 3.47 us  [shards(): pl.pallas_call(functools.partial(cross_kernel, near, far), out_shape=(plt...]
  transfers between devices with their start and end apart: 2 -> 2, of which waited for: 1 -> 1; matrix products, arithmetic and copies ran while one was open for 0% -> 0% of each run, Pallas kernels for 12% -> 11%
where the time goes in v6:
time: 53.3 us; the launch traced here: 53.2 us
  blocking collectives  34.5 us (65%)
  Pallas kernels  11.1 us (21%)
  starting transfers between devices  5.98 us (11%)
  waiting for transfers between devices  0.93 us (2%)
  between operations  0.67 us (1%)
    all_to_all x1, blocking collectives, shards(): got = lax.all_to_all(sent, NEAR, 0, 0, tiled=True)  19 us
    all_to_all x1, blocking collectives, shards(): got = lax.all_to_all(sent, FAR, 0, 0, tiled=True)  15.6 us
    pallas_call x1, Pallas kernels, shards(): pl.pallas_call(functools.partial(own_kernel, near, far), out_shape=(jax.S...  5.99 us
    pallas_call x1, Pallas kernels, shards(): pl.pallas_call(functools.partial(cross_kernel, near, far), out_shape=(plt...  3.47 us
    ppermute x1, starting transfers between devices, shards(): other = lax.ppermute(own, 'rep', SWAP)  3.29 us
    ppermute x1, starting transfers between devices, shards(): theirs = lax.ppermute(mine, 'rep', SWAP)  2.69 us
  transfers between devices with their start and end apart: 2, of which 1 were waited for; matrix products, arithmetic and copies ran while one was open for 0% of the time, Pallas kernels for 11%

profile of v6, /device:TPU:1, one launch (start us, length us, event | category | flops | bytes accessed | tf_op | source)
XLA Modules:
  0.0 53.2 jit_solution(3071836321901064865)
XLA Ops:
  0.6 3.3 %collective-permute-start = (bf16[50,128,256]{2,1,0:T(8,128)(2,1)}, bf16[50,128,256]{2,1,0:T(8,128)(2,1)S(1)}, u32[]{:S(2)}, u32[]{:S(2)}) collective-permute-start(bf16[50,128,256]{2,1,0:T(8,128)(2,1)} %bitcast.10), channel_id=1, source_target_pairs={{0,1},{1,0},{2,3},{3,2},{4,5},{5,4},{6,7},{7,6},{8,9},{9,8},{10,11... | collective-permute-start | bytes 9830408 | tf_op jit(solution)/shard_map/ppermute | solution.py:335
  3.9 0.0 copy-start
  3.9 6.0 %own.1 = (bf16[128,64,256]{2,1,0:T(8,128)(2,1)S(1)}, f32[3464,128]{1,0:T(8,128)S(1)}) custom-call(s32[1,128]{1,0:T(1,128)} %bitcast.8, s32[1,128]{1,0:T(1,128)} %bitcast.15, s32[1,128]{1,0:T(1,128)} %bitcast.16, s32[1,128]{1,0:T(1,128)} %bitcast.17, f32[128,256]{1,0:T(8,128)} %residual_in.1, f32[128,256]{1,0:T(8,128)} %error_in.1, f32[64,128]{1,0:T(8,128)} %bitcast.12, ...), custom_call_target="tpu_custom_call" | custom-call | flops 2000000000 | bytes 10000000 | tf_op jit(solution)/shard_map/own/pallas_call | solution.py:340
  9.9 0.0 collective-permute-done.other
  9.9 0.0 copy-done
  9.9 3.5 %cross.1 = (bf16[16,192,128]{2,1,0:T(8,128)(2,1)S(1)}, f32[3464,128]{1,0:T(8,128)S(1)}) custom-call(s32[1,128]{1,0:T(1,128)S(1)} %bitcast.9, bf16[128,64,256]{2,1,0:T(8,128)(2,1)S(1)} %get-tuple-element.9.left, f32[3464,128]{1,0:T(8,128)S(1)} %get-tuple-element.10.acc_in, ...), custom_call_target="tpu_custom_call", output_to_operand_aliasing={{1}: (2, {})} | custom-call | tf_op jit(solution)/shard_map/cross/pallas_call | solution.py:363
  13.4 19.0 %all_to_all.10.got = bf16[16,192,128]{2,1,0:T(8,128)(2,1)S(1)} all-to-all(bf16[16,192,128]{2,1,0:T(8,128)(2,1)S(1)} %get-tuple-element.11), channel_id=1, replica_groups=mesh['toa_0'=8,'toa_1'=4,'toa_2'=4,'rep'=2] {'toa_1','toa_2'}, dimensions={0} | all-to-all | bytes 1572864 | tf_op jit(solution)/shard_map/all_to_all | solution.py:375
  32.4 0.3 near_sum.1
  32.7 15.6 %all_to_all.11.got = bf16[8,48,128]{2,1,0:T(8,128)(2,1)S(1)} all-to-all(bf16[8,48,128]{2,1,0:T(8,128)(2,1)S(1)} %near_sum.1), channel_id=1, replica_groups=mesh['toa_0'=8,'toa_1'=4,'toa_2'=4,'rep'=2] {'toa_0'}, dimensions={0} | all-to-all | bytes 196608 | tf_op jit(solution)/shard_map/all_to_all | solution.py:384
  48.3 0.3 far_sum.1.mine_in
  48.5 2.7 %collective-permute-start.1 = (f32[160,128]{1,0:T(8,128)S(1)}, f32[160,128]{1,0:T(8,128)S(1)}, u32[]{:S(2)}, u32[]{:S(2)}) collective-permute-start(f32[160,128]{1,0:T(8,128)S(1)} %far_sum.1.mine_in), channel_id=1, source_target_pairs={{0,1},{1,0},{2,3},{3,2},{4,5},{5,4},{6,7},{7,6},{8,9},{9,8},{10,11... | collective-permute-start | bytes 245768 | tf_op jit(solution)/shard_map/ppermute | solution.py:392
  51.2 0.9 %collective-permute-done.1.theirs_in = f32[160,128]{1,0:T(8,128)S(1)} collective-permute-done((f32[160,128]{1,0:T(8,128)S(1)}, f32[160,128]{1,0:T(8,128)S(1)}, u32[]{:S(2)}, u32[]{:S(2)}) %collective-permute-start.1) | collective-permute-done | bytes 81952 | tf_op jit(solution)/shard_map/ppermute | solution.py:392
  52.1 1.0 %join.1 = (f32[50,1,100]{2,1,0:T(1,128)}, f32[1,50]{1,0:T(1,128)}, f32[128,256]{1,0:T(8,128)}) custom-call(f32[160,128]{1,0:T(8,128)S(1)} %far_sum.1.mine_in, f32[160,128]{1,0:T(8,128)S(1)} %collective-permute-done.1.theirs_in), custom_call_target="tpu_custom_call" | custom-call | tf_op jit(solution)/shard_map/join/pallas_call | solution.py:393
Async XLA Ops:
  0.6 9.3 %collective-permute-start = (bf16[50,128,256]{2,1,0:T(8,128)(2,1)}, bf16[50,128,256]{2,1,0:T(8,128)(2,1)S(1)}, u32[]{:S(2)}, u32[]{:S(2)}) collective-permute-start(bf16[50,128,256]{2,1,0:T(8,128)(2,1)} %bitcast.10), channel_id=1, source_target_pairs={{0,1},{1,0},{2,3},{3,2},{4,5},{5,4},{6,7},{7,6},{8,9},{9,8},{10,11... | collective-permute-start | bytes 9830408 | tf_op jit(solution)/shard_map/ppermute | solution.py:335
  3.9 6.0 %copy-start = (s32[128]{0:T(128)S(1)}, s32[128]{0:T(128)}, u32[]{:S(2)}) copy-start(s32[128]{0:T(128)} %param.14) | copy-start | bytes 1540
  48.5 3.6 %collective-permute-start.1 = (f32[160,128]{1,0:T(8,128)S(1)}, f32[160,128]{1,0:T(8,128)S(1)}, u32[]{:S(2)}, u32[]{:S(2)}) collective-permute-start(f32[160,128]{1,0:T(8,128)S(1)} %far_sum.1.mine_in), channel_id=1, source_target_pairs={{0,1},{1,0},{2,3},{3,2},{4,5},{5,4},{6,7},{7,6},{8,9},{9,8},{10,11... | collective-permute-start | bytes 245768 | tf_op jit(solution)/shard_map/ppermute | solution.py:392

commit v7 on v6

--- a/solution.py
+++ b/solution.py
@@ -189,7 +189,7 @@
             acc[pl.ds(base, WIDE), :cols] += value[:WIDE]
         return carry
 
-    lax.fori_loop(0, tiles // GROUP, turn, 0)
+    lax.fori_loop(0, tiles // GROUP, turn, 0, unroll=tiles // GROUP)
 
     lane = iota((WIDE, LANES), 1)
     spare = (lane >= USED) & (lane < USED + PIECE)
@@ -210,8 +210,8 @@
         out[n] = acc[pl.ds(pl.multiple_of(n * block, 8), message), :].astype(BF16)
         return carry
 
-    lax.fori_loop(0, near, fold, 0, unroll=4)
-    lax.fori_loop(0, near, convert, 0, unroll=2)
+    lax.fori_loop(0, near, fold, 0, unroll=8)
+    lax.fori_loop(0, near, convert, 0, unroll=4)
 
 
 def near_kernel(far, got, out, total):

time: 53.3 us -> 52.2 us (0.979)
  Pallas kernels: 11.1 us -> 9.88 us
    pallas_call x1, Pallas kernels: 3.47 us -> 2.29 us  [shards(): pl.pallas_call(functools.partial(cross_kernel, near, far), out_shape=(plt...]
  transfers between devices with their start and end apart: 2 -> 2, of which waited for: 1 -> 1; matrix products, arithmetic and copies ran while one was open for 0% -> 0% of each run, Pallas kernels for 11% -> 12%
where the time goes in v7:
time: 52.2 us; the launch traced here: 52 us
  blocking collectives  34.5 us (66%)
  Pallas kernels  9.88 us (19%)
  starting transfers between devices  5.98 us (11%)
  waiting for transfers between devices  0.93 us (2%)
  between operations  0.67 us (1%)
    all_to_all x1, blocking collectives, shards(): got = lax.all_to_all(sent, NEAR, 0, 0, tiled=True)  19 us
    all_to_all x1, blocking collectives, shards(): got = lax.all_to_all(sent, FAR, 0, 0, tiled=True)  15.5 us
    pallas_call x1, Pallas kernels, shards(): pl.pallas_call(functools.partial(own_kernel, near, far), out_shape=(jax.S...  5.99 us
    ppermute x1, starting transfers between devices, shards(): other = lax.ppermute(own, 'rep', SWAP)  3.29 us
    ppermute x1, starting transfers between devices, shards(): theirs = lax.ppermute(mine, 'rep', SWAP)  2.69 us
    pallas_call x1, Pallas kernels, shards(): pl.pallas_call(functools.partial(cross_kernel, near, far), out_shape=(plt...  2.29 us
  transfers between devices with their start and end apart: 2, of which 1 were waited for; matrix products, arithmetic and copies ran while one was open for 0% of the time, Pallas kernels for 12%

profile of v7, /device:TPU:1, one launch (start us, length us, event | category | flops | bytes accessed | tf_op | source)
XLA Modules:
  0.0 52.0 jit_solution(16596185067534338404)
XLA Ops:
  0.6 3.3 %collective-permute-start = (bf16[50,128,256]{2,1,0:T(8,128)(2,1)}, bf16[50,128,256]{2,1,0:T(8,128)(2,1)S(1)}, u32[]{:S(2)}, u32[]{:S(2)}) collective-permute-start(bf16[50,128,256]{2,1,0:T(8,128)(2,1)} %bitcast.10), channel_id=1, source_target_pairs={{0,1},{1,0},{2,3},{3,2},{4,5},{5,4},{6,7},{7,6},{8,9},{9,8},{10,11... | collective-permute-start | bytes 9830408 | tf_op jit(solution)/shard_map/ppermute | solution.py:335
  3.9 0.0 copy-start
  3.9 6.0 %own.1 = (bf16[128,64,256]{2,1,0:T(8,128)(2,1)S(1)}, f32[3464,128]{1,0:T(8,128)S(1)}) custom-call(s32[1,128]{1,0:T(1,128)} %bitcast.8, s32[1,128]{1,0:T(1,128)} %bitcast.15, s32[1,128]{1,0:T(1,128)} %bitcast.16, s32[1,128]{1,0:T(1,128)} %bitcast.17, f32[128,256]{1,0:T(8,128)} %residual_in.1, f32[128,256]{1,0:T(8,128)} %error_in.1, f32[64,128]{1,0:T(8,128)} %bitcast.12, ...), custom_call_target="tpu_custom_call" | custom-call | flops 2000000000 | bytes 10000000 | tf_op jit(solution)/shard_map/own/pallas_call | solution.py:340
  9.9 0.0 collective-permute-done.other
  9.9 0.0 copy-done
  9.9 2.3 %cross.1 = (bf16[16,192,128]{2,1,0:T(8,128)(2,1)S(1)}, f32[3464,128]{1,0:T(8,128)S(1)}) custom-call(s32[1,128]{1,0:T(1,128)S(1)} %bitcast.9, bf16[128,64,256]{2,1,0:T(8,128)(2,1)S(1)} %get-tuple-element.9.left, f32[3464,128]{1,0:T(8,128)S(1)} %get-tuple-element.10.acc_in, ...), custom_call_target="tpu_custom_call", output_to_operand_aliasing={{1}: (2, {})} | custom-call | tf_op jit(solution)/shard_map/cross/pallas_call | solution.py:363
  12.2 19.0 %all_to_all.10.got = bf16[16,192,128]{2,1,0:T(8,128)(2,1)S(1)} all-to-all(bf16[16,192,128]{2,1,0:T(8,128)(2,1)S(1)} %get-tuple-element.11), channel_id=1, replica_groups=mesh['toa_0'=8,'toa_1'=4,'toa_2'=4,'rep'=2] {'toa_1','toa_2'}, dimensions={0} | all-to-all | bytes 1572864 | tf_op jit(solution)/shard_map/all_to_all | solution.py:375
  31.2 0.3 near_sum.1
  31.5 15.5 %all_to_all.11.got = bf16[8,48,128]{2,1,0:T(8,128)(2,1)S(1)} all-to-all(bf16[8,48,128]{2,1,0:T(8,128)(2,1)S(1)} %near_sum.1), channel_id=1, replica_groups=mesh['toa_0'=8,'toa_1'=4,'toa_2'=4,'rep'=2] {'toa_0'}, dimensions={0} | all-to-all | bytes 196608 | tf_op jit(solution)/shard_map/all_to_all | solution.py:384
  47.1 0.3 far_sum.1.mine_in
  47.4 2.7 %collective-permute-start.1 = (f32[160,128]{1,0:T(8,128)S(1)}, f32[160,128]{1,0:T(8,128)S(1)}, u32[]{:S(2)}, u32[]{:S(2)}) collective-permute-start(f32[160,128]{1,0:T(8,128)S(1)} %far_sum.1.mine_in), channel_id=1, source_target_pairs={{0,1},{1,0},{2,3},{3,2},{4,5},{5,4},{6,7},{7,6},{8,9},{9,8},{10,11... | collective-permute-start | bytes 245768 | tf_op jit(solution)/shard_map/ppermute | solution.py:392
  50.0 0.9 %collective-permute-done.1.theirs_in = f32[160,128]{1,0:T(8,128)S(1)} collective-permute-done((f32[160,128]{1,0:T(8,128)S(1)}, f32[160,128]{1,0:T(8,128)S(1)}, u32[]{:S(2)}, u32[]{:S(2)}) %collective-permute-start.1) | collective-permute-done | bytes 81952 | tf_op jit(solution)/shard_map/ppermute | solution.py:392
  51.0 1.0 %join.1 = (f32[50,1,100]{2,1,0:T(1,128)}, f32[1,50]{1,0:T(1,128)}, f32[128,256]{1,0:T(8,128)}) custom-call(f32[160,128]{1,0:T(8,128)S(1)} %far_sum.1.mine_in, f32[160,128]{1,0:T(8,128)S(1)} %collective-permute-done.1.theirs_in), custom_call_target="tpu_custom_call" | custom-call | tf_op jit(solution)/shard_map/join/pallas_call | solution.py:393
Async XLA Ops:
  0.6 9.3 %collective-permute-start = (bf16[50,128,256]{2,1,0:T(8,128)(2,1)}, bf16[50,128,256]{2,1,0:T(8,128)(2,1)S(1)}, u32[]{:S(2)}, u32[]{:S(2)}) collective-permute-start(bf16[50,128,256]{2,1,0:T(8,128)(2,1)} %bitcast.10), channel_id=1, source_target_pairs={{0,1},{1,0},{2,3},{3,2},{4,5},{5,4},{6,7},{7,6},{8,9},{9,8},{10,11... | collective-permute-start | bytes 9830408 | tf_op jit(solution)/shard_map/ppermute | solution.py:335
  3.9 6.0 %copy-start = (s32[128]{0:T(128)S(1)}, s32[128]{0:T(128)}, u32[]{:S(2)}) copy-start(s32[128]{0:T(128)} %param.14) | copy-start | bytes 1540
  47.4 3.6 %collective-permute-start.1 = (f32[160,128]{1,0:T(8,128)S(1)}, f32[160,128]{1,0:T(8,128)S(1)}, u32[]{:S(2)}, u32[]{:S(2)}) collective-permute-start(f32[160,128]{1,0:T(8,128)S(1)} %far_sum.1.mine_in), channel_id=1, source_target_pairs={{0,1},{1,0},{2,3},{3,2},{4,5},{5,4},{6,7},{7,6},{8,9},{9,8},{10,11... | collective-permute-start | bytes 245768 | tf_op jit(solution)/shard_map/ppermute | solution.py:392

commit v8 on v7

--- a/solution.py
+++ b/solution.py
@@ -257,7 +257,13 @@
     out[SECOND:, :] = dot(put, got[:, :near, :].reshape(tiles, LANES), ((0,), (0,)))
 
 
-def join_kernel(mine_in, theirs_in, gram, proj, white, mine_t, theirs_t):
+def join_kernel(mine_in, theirs_in, gram, proj, white, mine_t, theirs_t, sems):
+    core = lax.axis_index("rep")
+    copies = []
+    for i, (half, at) in enumerate(((mine_in, core), (theirs_in, 1 - core))):
+        to = white.at[:, pl.ds(pl.multiple_of(at * LANES, LANES), LANES)]
+        copies.append(pltpu.make_async_copy(half.at[SECOND:, :], to, sems.at[i]))
+        copies[-1].start()
     lane, row = iota((SECOND, LANES), 1), iota((SECOND, LANES), 0)
     mine = mine_in[1 : SECOND + 1, :]
 
@@ -292,11 +298,6 @@
             under += [(mine, PART, low), (theirs_1, 0, high)]
         gram[:PART, 0, :] = laid(top)[:PART, : 4 * PART]
         gram[PART:, 0, :] = laid(under)[:PART, : 4 * PART]
-        halves = (mine_in, theirs_in) if own == 0 else (theirs_in, mine_in)
-        for i, half in enumerate(halves):
-            white[:, i * LANES : (i + 1) * LANES] = half[SECOND:, :]
-
-    core = lax.axis_index("rep")
 
     @pl.when(core == 0)
     def _():
@@ -308,6 +309,8 @@
 
     sums = joined(mine_in[:SECOND, :])
     proj[...] = laid([(sums, OWN + 1, 0), (sums, OWN2 + 1, PART)])[:1, : 2 * PART]
+    for copy in copies:
+        copy.wait()
 
 
 def vmem(n):
@@ -398,8 +401,8 @@
             jax.ShapeDtypeStruct((tiles, rows), F32),
         ),
         in_specs=vmem(2),
-        out_specs=tuple(vmem(3)),
-        scratch_shapes=[pltpu.VMEM((LANES, LANES), F32)] * 2,
+        out_specs=tuple(vmem(2) + [HBM]),
+        scratch_shapes=[pltpu.VMEM((LANES, LANES), F32)] * 2 + [pltpu.SemaphoreType.DMA((2,))],
         name="join",
     )(near_by(mine), near_by(theirs))
     return jnp.transpose(gram, (1, 2, 0)), projection, whitened

time: 52.2 us -> 52.4 us (level)
  transfers between devices with their start and end apart: 2 -> 2, of which waited for: 1 -> 1; matrix products, arithmetic and copies ran while one was open for 0% -> 0% of each run, Pallas kernels for 12% -> 11%
where the time goes in v8:
time: 52.4 us; the launch traced here: 52.3 us
  blocking collectives  34.5 us (66%)
  Pallas kernels  10.2 us (19%)
  starting transfers between devices  5.97 us (11%)
  waiting for transfers between devices  0.93 us (2%)
  between operations  0.67 us (1%)
    all_to_all x1, blocking collectives, shards(): got = lax.all_to_all(sent, NEAR, 0, 0, tiled=True)  19 us
    all_to_all x1, blocking collectives, shards(): got = lax.all_to_all(sent, FAR, 0, 0, tiled=True)  15.6 us
    pallas_call x1, Pallas kernels, shards(): pl.pallas_call(functools.partial(own_kernel, near, far), out_shape=(jax.S...  5.99 us
    ppermute x1, starting transfers between devices, shards(): other = lax.ppermute(own, 'rep', SWAP)  3.29 us
    ppermute x1, starting transfers between devices, shards(): theirs = lax.ppermute(mine, 'rep', SWAP)  2.68 us
    pallas_call x1, Pallas kernels, shards(): pl.pallas_call(functools.partial(cross_kernel, near, far), out_shape=(plt...  2.3 us
    pallas_call x1, Pallas kernels, shards(): pl.pallas_call(join_kernel, out_shape=(jax.ShapeDtypeStruct((cols, 1, 2 *...  1.28 us
  transfers between devices with their start and end apart: 2, of which 1 were waited for; matrix products, arithmetic and copies ran while one was open for 0% of the time, Pallas kernels for 11%

profile of v8, /device:TPU:1, one launch (start us, length us, event | category | flops | bytes accessed | tf_op | source)
XLA Modules:
  0.0 52.3 jit_solution(15541949419033578277)
XLA Ops:
  0.6 3.3 %collective-permute-start = (bf16[50,128,256]{2,1,0:T(8,128)(2,1)}, bf16[50,128,256]{2,1,0:T(8,128)(2,1)S(1)}, u32[]{:S(2)}, u32[]{:S(2)}) collective-permute-start(bf16[50,128,256]{2,1,0:T(8,128)(2,1)} %bitcast.10), channel_id=1, source_target_pairs={{0,1},{1,0},{2,3},{3,2},{4,5},{5,4},{6,7},{7,6},{8,9},{9,8},{10,11... | collective-permute-start | bytes 9830408 | tf_op jit(solution)/shard_map/ppermute | solution.py:338
  3.9 0.0 copy-start
  3.9 6.0 %own.1 = (bf16[128,64,256]{2,1,0:T(8,128)(2,1)S(1)}, f32[3464,128]{1,0:T(8,128)S(1)}) custom-call(s32[1,128]{1,0:T(1,128)} %bitcast.8, s32[1,128]{1,0:T(1,128)} %bitcast.15, s32[1,128]{1,0:T(1,128)} %bitcast.16, s32[1,128]{1,0:T(1,128)} %bitcast.17, f32[128,256]{1,0:T(8,128)} %residual_in.1, f32[128,256]{1,0:T(8,128)} %error_in.1, f32[64,128]{1,0:T(8,128)} %bitcast.12, ...), custom_call_target="tpu_custom_call" | custom-call | flops 2000000000 | bytes 10000000 | tf_op jit(solution)/shard_map/own/pallas_call | solution.py:343
  9.9 0.0 collective-permute-done.other
  9.9 0.0 copy-done
  9.9 2.3 %cross.1 = (bf16[16,192,128]{2,1,0:T(8,128)(2,1)S(1)}, f32[3464,128]{1,0:T(8,128)S(1)}) custom-call(s32[1,128]{1,0:T(1,128)S(1)} %bitcast.9, bf16[128,64,256]{2,1,0:T(8,128)(2,1)S(1)} %get-tuple-element.9.left, f32[3464,128]{1,0:T(8,128)S(1)} %get-tuple-element.10.acc_in, ...), custom_call_target="tpu_custom_call", output_to_operand_aliasing={{1}: (2, {})} | custom-call | tf_op jit(solution)/shard_map/cross/pallas_call | solution.py:366
  12.2 19.0 %all_to_all.10.got = bf16[16,192,128]{2,1,0:T(8,128)(2,1)S(1)} all-to-all(bf16[16,192,128]{2,1,0:T(8,128)(2,1)S(1)} %get-tuple-element.11), channel_id=1, replica_groups=mesh['toa_0'=8,'toa_1'=4,'toa_2'=4,'rep'=2] {'toa_1','toa_2'}, dimensions={0} | all-to-all | bytes 1572864 | tf_op jit(solution)/shard_map/all_to_all | solution.py:378
  31.2 0.3 near_sum.1
  31.5 15.6 %all_to_all.11.got = bf16[8,48,128]{2,1,0:T(8,128)(2,1)S(1)} all-to-all(bf16[8,48,128]{2,1,0:T(8,128)(2,1)S(1)} %near_sum.1), channel_id=1, replica_groups=mesh['toa_0'=8,'toa_1'=4,'toa_2'=4,'rep'=2] {'toa_0'}, dimensions={0} | all-to-all | bytes 196608 | tf_op jit(solution)/shard_map/all_to_all | solution.py:387
  47.1 0.3 far_sum.1.mine_in
  47.4 2.7 %collective-permute-start.1 = (f32[160,128]{1,0:T(8,128)S(1)}, f32[160,128]{1,0:T(8,128)S(1)}, u32[]{:S(2)}, u32[]{:S(2)}) collective-permute-start(f32[160,128]{1,0:T(8,128)S(1)} %far_sum.1.mine_in), channel_id=1, source_target_pairs={{0,1},{1,0},{2,3},{3,2},{4,5},{5,4},{6,7},{7,6},{8,9},{9,8},{10,11... | collective-permute-start | bytes 245768 | tf_op jit(solution)/shard_map/ppermute | solution.py:395
  50.1 0.9 %collective-permute-done.1.theirs_in = f32[160,128]{1,0:T(8,128)S(1)} collective-permute-done((f32[160,128]{1,0:T(8,128)S(1)}, f32[160,128]{1,0:T(8,128)S(1)}, u32[]{:S(2)}, u32[]{:S(2)}) %collective-permute-start.1) | collective-permute-done | bytes 81952 | tf_op jit(solution)/shard_map/ppermute | solution.py:395
  51.0 1.3 %join.1 = (f32[50,1,100]{2,1,0:T(1,128)}, f32[1,50]{1,0:T(1,128)}, f32[128,256]{1,0:T(8,128)}) custom-call(f32[160,128]{1,0:T(8,128)S(1)} %far_sum.1.mine_in, f32[160,128]{1,0:T(8,128)S(1)} %collective-permute-done.1.theirs_in), custom_call_target="tpu_custom_call" | custom-call | tf_op jit(solution)/shard_map/join/pallas_call | solution.py:396
Async XLA Ops:
  0.6 9.3 %collective-permute-start = (bf16[50,128,256]{2,1,0:T(8,128)(2,1)}, bf16[50,128,256]{2,1,0:T(8,128)(2,1)S(1)}, u32[]{:S(2)}, u32[]{:S(2)}) collective-permute-start(bf16[50,128,256]{2,1,0:T(8,128)(2,1)} %bitcast.10), channel_id=1, source_target_pairs={{0,1},{1,0},{2,3},{3,2},{4,5},{5,4},{6,7},{7,6},{8,9},{9,8},{10,11... | collective-permute-start | bytes 9830408 | tf_op jit(solution)/shard_map/ppermute | solution.py:338
  3.9 6.0 %copy-start = (s32[128]{0:T(128)S(1)}, s32[128]{0:T(128)}, u32[]{:S(2)}) copy-start(s32[128]{0:T(128)} %param.14) | copy-start | bytes 1540
  47.4 3.6 %collective-permute-start.1 = (f32[160,128]{1,0:T(8,128)S(1)}, f32[160,128]{1,0:T(8,128)S(1)}, u32[]{:S(2)}, u32[]{:S(2)}) collective-permute-start(f32[160,128]{1,0:T(8,128)S(1)} %far_sum.1.mine_in), channel_id=1, source_target_pairs={{0,1},{1,0},{2,3},{3,2},{4,5},{5,4},{6,7},{7,6},{8,9},{9,8},{10,11... | collective-permute-start | bytes 245768 | tf_op jit(solution)/shard_map/ppermute | solution.py:395
